TPU v7x, 256 devices: a 8x8x2 block of a 8x8x16 slice. The times are simulated.
256 devices in a mesh: groups: 2 (over z), seq: 128 (over y, x, core).
Axes of the slice: x: 8, y: 8, z: 2, core: 2. Of those that a mesh axis runs over, the one named last changes fastest.
The devices are a block of a 8x8x16 slice.
Arguments:
- hidden: bfloat16 [8192, 3072], P(('groups', 'seq')), parts along dimension 0, may hold values from -6 to 6
- queries: bfloat16 [8192, 3072], P(('groups', 'seq')), parts along dimension 0, may hold values from -6 to 6
- key_rows: bfloat16 [8192, 3072], P(('groups', 'seq')), parts along dimension 0, may hold values from -6 to 6
- values: bfloat16 [8192, 3072], P(('groups', 'seq')), parts along dimension 0, may hold values from -12 to 12
- query_gain: float32 [2, 128], replicated, may hold values from 0.6 to 5
- key_gain: float32 [2, 128], replicated, may hold values from 0.6 to 5
- gate_table: bfloat16 [64, 2, 3072], P('groups'), parts along dimension 0, may hold values from -6 to 6
- segment: int32 [8192], P(('groups', 'seq')), parts along dimension 0, may hold values from 0 to 31, as said below
- text_count: int32 [64], P('groups'), parts along dimension 0, may hold values from 1 to 64
Outputs:
- mixed: bfloat16 [8192, 3072], P(('groups', 'seq')), parts along dimension 0
There are 2 independent parts, one for each index of `groups`. A program takes and returns all parts, laid end to end along the dimension named above; an argument that names none is the same for every part. Nothing has to cross between parts.
Inputs may be any that keep to these rules, and one draw needn't show every extreme that they name: `segment`: one device holds at most 2 tokens of one request; in every draw some two requests 2 j and 2 j + 1 get exactly 2 tokens from every device. Tokens of one request may lie anywhere on the devices.
All inputs are finite; a program needn't handle non-finite values.
Results may differ from a plain program's by a relative error of at most 0.012.
The roundings to bfloat16 on the way count: a program that leaves them out, or rounds other values in their place, can miss the bound.
Values may be sent and summed in bfloat16 or wider, within the bound.
A program may use at most 64 MiB of HBM per device.

v0:
```python
import math

import jax
import jax.numpy as jnp
from jax import lax
from jax.sharding import Mesh
from jax.sharding import PartitionSpec as P

HEAD_DIM = 128
SEQ = ("seq_0", "seq_1", "seq_2")
GROUPS_SEQ = ("groups", "seq_0", "seq_1", "seq_2")


EPSILON = 1e-06
MASKED = -1e30


def in_order(parts, dim):
    dims = list(parts.shape[1:])
    dims[dim] *= parts.shape[0]
    return jnp.moveaxis(parts, 0, dim).reshape(dims)


def gather_in_order(array, axes, order):
    parts = array
    for k in order:
        parts = lax.all_gather(parts, axes[k])
    done = order[::-1]
    back = [done.index(k) for k in range(len(axes))]
    parts = parts.transpose(*back, *range(len(axes), parts.ndim))
    return parts.reshape(-1, *array.shape)


def whole_of(array, axes, order, dim):
    return in_order(gather_in_order(array, axes, order), dim)


def head_norm(rows_in, gains, stream):
    row_count = rows_in.shape[0]
    per_head = rows_in.astype(jnp.float32).reshape(row_count, -1, HEAD_DIM)
    inverse = lax.rsqrt(jnp.mean(per_head * per_head, axis=-1, keepdims=True) + EPSILON)
    gain_rows = jnp.where((stream == 0)[:, None], gains[0][None, :], gains[1][None, :])
    return (per_head * inverse * gain_rows[:, None, :]).astype(jnp.bfloat16).reshape(row_count, -1)


def attend(query_block, block_segment, key_data, value_data, key_segment):
    scores = jnp.einsum(
        "qhd,khd->hqk", query_block, key_data, preferred_element_type=jnp.float32
    ) * (1.0 / math.sqrt(HEAD_DIM))
    allowed = (block_segment[:, None] == key_segment[None, :])[None, :, :]
    scores = jnp.where(allowed, scores, MASKED)
    largest = jnp.max(scores, axis=-1, keepdims=True)
    weights = jnp.exp(scores - largest)
    weights = (weights / jnp.sum(weights, axis=-1, keepdims=True)).astype(jnp.bfloat16)
    return jnp.einsum(
        "hqk,khd->qhd", weights, value_data, preferred_element_type=jnp.float32
    ).astype(jnp.bfloat16)


def per_device(
    hidden, queries, key_rows, values, query_gain, key_gain, gate_table, segment, text_count
):
    tok_rows = hidden.shape[0]
    width_all = hidden.shape[1]
    devices = lax.axis_size(SEQ)
    requests = text_count.shape[0]
    seg_hot = (segment[:, None] == jnp.arange(requests, dtype=jnp.int32)[None, :]).astype(jnp.int32)
    local_counts = jnp.sum(seg_hot, axis=0)
    all_counts = whole_of(local_counts[None, :], (("seq_0", "seq_1"), "seq_2"), (0, 1), 0)
    lower_rows = (jnp.arange(devices, dtype=jnp.int32) < lax.axis_index(SEQ)).astype(jnp.int32)
    before = jnp.sum(all_counts * lower_rows[:, None], axis=0)
    position = jnp.sum((jnp.cumsum(seg_hot, axis=0) - seg_hot + before[None, :]) * seg_hot, axis=1)
    text_limit = jnp.sum(seg_hot * text_count[None, :], axis=1)
    stream = (position >= text_limit).astype(jnp.int32)
    query_normed = head_norm(queries, query_gain, stream)
    key_normed = head_norm(key_rows, key_gain, stream)
    groups = 8
    pair_merge = 2
    slices = devices // groups
    cap_rows = 4 * tok_rows // devices + max(1, tok_rows // devices)
    bucket_rows = cap_rows * pair_merge
    head_cols = width_all // groups
    owner_slice = segment // pair_merge
    owner_hot = (owner_slice[:, None] == jnp.arange(slices, dtype=jnp.int32)[None, :]).astype(
        jnp.int32
    )
    owner_rank = jnp.sum((jnp.cumsum(owner_hot, axis=0) - owner_hot) * owner_hot, axis=1)
    slot_place = owner_slice * bucket_rows + owner_rank
    bucket_index = (
        jnp.full((slices * bucket_rows,), tok_rows, jnp.int32)
        .at[slot_place]
        .set(jnp.arange(tok_rows, dtype=jnp.int32))
    )
    stacked = jnp.concatenate(
        [
            query_normed.reshape(tok_rows, groups, head_cols),
            key_normed.reshape(tok_rows, groups, head_cols),
            values.reshape(tok_rows, groups, head_cols),
        ],
        axis=2,
    ).transpose(1, 0, 2)
    outgoing = jnp.take(stacked, bucket_index, axis=1, mode="fill", fill_value=0).reshape(
        devices, bucket_rows, 3 * head_cols
    )
    slot_segment = jnp.take(segment, bucket_index, axis=0, mode="fill", fill_value=-1)
    segment_out = jnp.broadcast_to(slot_segment[None, :], (groups, slices * bucket_rows)).reshape(
        devices, bucket_rows
    )
    arrived, arrived_segment = (
        lax.all_to_all(outgoing, SEQ, split_axis=0, concat_axis=0, tiled=True),
        lax.all_to_all(segment_out, SEQ, split_axis=0, concat_axis=0, tiled=True),
    )
    slot_count = devices * bucket_rows
    per_head = head_cols // HEAD_DIM
    slot_data = arrived.reshape(slot_count, 3 * head_cols)
    query_all = slot_data[:, :head_cols].reshape(slot_count, per_head, HEAD_DIM)
    key_all = slot_data[:, head_cols : 2 * head_cols].reshape(slot_count, per_head, HEAD_DIM)
    value_all = slot_data[:, 2 * head_cols :].reshape(slot_count, per_head, HEAD_DIM)
    key_segment = arrived_segment.reshape(slot_count)
    block_rows = 512

    def one_block(first_row):
        return attend(query_all, key_segment, key_all, value_all, key_segment)

    results = lax.map(one_block, jnp.arange(slot_count // block_rows, dtype=jnp.int32) * block_rows)
    returning = results.reshape(devices, bucket_rows, head_cols)
    returned = lax.all_to_all(returning, SEQ, split_axis=0, concat_axis=0, tiled=True)
    returned = returned.reshape(groups, slices * bucket_rows, head_cols)
    attention = (
        jnp.take(returned, slot_place, axis=1).transpose(1, 0, 2).reshape(tok_rows, width_all)
    )
    gate_rows = jnp.take(gate_table.reshape(requests * 2, width_all), segment * 2 + stream, axis=0)
    mixed = hidden.astype(jnp.float32) + gate_rows.astype(jnp.float32) * attention.astype(
        jnp.float32
    )
    return mixed.astype(jnp.bfloat16)


def solution(mesh):
    finer = Mesh(
        mesh.devices.reshape(mesh.shape["groups"], 8, 8, 2), ("groups", "seq_0", "seq_1", "seq_2")
    )
    placed = (
        P(GROUPS_SEQ, None),
        P(GROUPS_SEQ, None),
        P(GROUPS_SEQ, None),
        P(GROUPS_SEQ, None),
        P(),
        P(),
        P("groups", None, None),
        P(GROUPS_SEQ),
        P("groups"),
    )
    return jax.shard_map(
        per_device, mesh=finer, in_specs=placed, out_specs=P(GROUPS_SEQ, None), check_vma=False
    )
```

profile of v0, /device:TPU:513, one launch (start us, length us, event | category | flops | bytes accessed | tf_op | source)
XLA Modules:
  0.0 147.7 jit_solution(7185551694400107522)
XLA Ops:
  0.0 0.7 and_select_fusion
  1.1 0.7 compare_and_fusion.1
  1.7 0.7 scatter_custom_fusion
  2.4 1.4 gather_fusion.2
  4.0 0.6 broadcast_in_dim.167
  4.6 27.4 %all-to-all-start.1 = ((s32[128,1,4]{2,1,0:T(1,128)}), s32[128,1,4]{2,1,0:T(1,128)S(1)}, u32[]{:S(2)}, u32[]{:S(2)}) async-start(s32[128,1,4]{2,1,0:T(1,128)} %bitcast.11), calls=%async_computation.1 | async-start | bytes 131072 | tf_op jit(solution)/shard_map/all_to_all | solution.py:111
  32.0 0.7 fusion.15
  32.8 1.0 copy.44
  34.0 0.7 dynamic-slice
  35.6 22.4 %all-reduce = s32[2048]{0:T(1024)S(1)} all-reduce(s32[2048]{0:T(1024)S(1)} %dynamic-update-slice), channel_id=2, replica_groups=mesh['groups'=2,'seq_0'=8,'seq_1'=8,'seq_2'=2] {'seq_0','seq_1'}, use_global_device_ids=true, to_apply=%add | all-reduce | flops 2048 | bytes 16384
  58.1 7.1 %all-gather.1 = s32[128,1,32]{2,0,1:T(8,128)S(1)} all-gather(s32[64,1,32]{2,0,1:T(8,128)S(1)} %reshape.274), channel_id=3, replica_groups=mesh['groups'=2,'seq_0'=8,'seq_1'=8,'seq_2'=2] {'seq_2'}, dimensions={0}, use_global_device_ids=true | all-gather | bytes 24576 | tf_op jit(solution)/shard_map/all_gather | solution.py:27
  66.5 0.7 copy-done.2
  68.0 0.7 gather_fusion.1
  69.4 1.6 %broadcast_select_fusion = bf16[128,4,1152]{2,1,0:T(4,128)(2,1)} fusion(bf16[128,4,1152]{2,1,0:T(4,128)(2,1)S(1)} %gather.20, pred[128,4]{1,0:T(8,128)(4,1)S(1)} %bitcast.66), kind=kLoop, calls=%fused_computation.16 | loop fusion | flops 589824 | bytes 2359808 | tf_op jit(solution)/shard_map/jit(_take)/select_n | solution.py:102
  71.0 8.9 %all-to-all-start = ((bf16[128,4,1152]{2,1,0:T(4,128)(2,1)}), bf16[128,4,1152]{2,1,0:T(4,128)(2,1)S(1)}, u32[]{:S(2)}, u32[]{:S(2)}) async-start(bf16[128,4,1152]{2,1,0:T(4,128)(2,1)} %broadcast_select_fusion), calls=%async_computation | async-start | bytes 2359296 | tf_op jit(solution)/shard_map/all_to_all | solution.py:110
  80.4 0.8 reduce.4
  81.6 30.8 %all-to-all-done = bf16[128,4,1152]{2,1,0:T(4,128)(2,1)S(1)} async-done(((bf16[128,4,1152]{2,1,0:T(4,128)(2,1)}), bf16[128,4,1152]{2,1,0:T(4,128)(2,1)S(1)}, u32[]{:S(2)}, u32[]{:S(2)}) %all-to-all-start) | async-done | bytes 1179680 | tf_op jit(solution)/shard_map/all_to_all | solution.py:110
  113.5 3.0 %fusion.22 = (f32[3,512]{1,0:T(4,128)S(1)}, f32[3,512,512]{1,2,0:T(8,128)}) fusion(pred[512,512]{0,1:T(8,128)(4,1)S(1)} %broadcast_compare_fusion, bf16[512,3,128]{0,2,1:T(8,128)(2,1)S(1)} %bitcast.62, bf16[512,3,128]{0,2,1:T(8,128)(2,1)S(1)} %bitcast.63), kind=kOutput, calls=%fused_computation.69 | convolution fusion | flops 204472832 | bytes 4200448 | tf_op jit(solution)/shard_map/while/body/eval_jaxpr/sub | solution.py:53
  116.5 2.3 %fusion.7 = bf16[512,3,128]{0,2,1:T(8,128)(2,1)S(1)} fusion(bf16[512,3,128]{0,2,1:T(8,128)(2,1)S(1)} %bitcast.61, f32[3,512,512]{1,2,0:T(8,128)} %get-tuple-element.42, f32[3,512]{1,0:T(4,128)S(1)} %get-tuple-element.41), kind=kOutput, calls=%fused_computation.15 | convolution fusion | flops 203096064 | bytes 3938304 | tf_op jit(solution)/shard_map/while/body/eval_jaxpr/hqk,khd->qhd/dot_general | solution.py:55
  119.1 1.1 reshape.231
  120.2 8.5 %all-to-all-start.2 = ((bf16[128,4,384]{2,1,0:T(4,128)(2,1)}), bf16[128,4,384]{2,1,0:T(4,128)(2,1)S(1)}, u32[]{:S(2)}, u32[]{:S(2)}) async-start(bf16[128,4,384]{2,1,0:T(4,128)(2,1)} %reshape.231), calls=%async_computation.2 | async-start | bytes 786432 | tf_op jit(solution)/shard_map/all_to_all | solution.py:127
  128.9 0.7 gather_fusion
  129.6 16.1 %all-to-all-done.2 = bf16[128,4,384]{2,1,0:T(4,128)(2,1)S(1)} async-done(((bf16[128,4,384]{2,1,0:T(4,128)(2,1)}), bf16[128,4,384]{2,1,0:T(4,128)(2,1)S(1)}, u32[]{:S(2)}, u32[]{:S(2)}) %all-to-all-start.2) | async-done | bytes 393248 | tf_op jit(solution)/shard_map/all_to_all | solution.py:127
  146.8 0.8 add_convert_fusion
  (79 shorter events, 7.0 us)
Async XLA Ops:
  0.0 34.0 %copy-start.8 = (u32[256]{0:T(256)S(1)}, u32[256]{0:T(256)}, u32[]{:S(2)}) copy-start(u32[256]{0:T(256)} %constant.133) | copy-start | bytes 3076
  0.0 33.8 %copy-start = (s32[32]{0:T(128)S(1)}, s32[32]{0:T(128)}, u32[]{:S(2)}) copy-start(s32[32]{0:T(128)} %param.16) | copy-start | bytes 388
  0.0 33.8 %copy-start.7 = (s32[32]{0:T(128)S(1)}, s32[32]{0:T(128)}, u32[]{:S(2)}) copy-start(s32[32]{0:T(128)} %param.17) | copy-start | bytes 388
  0.0 65.2 %copy-start.5 = (f32[2,128]{1,0:T(2,128)S(1)}, f32[2,128]{1,0:T(2,128)}, u32[]{:S(2)}) copy-start(f32[2,128]{1,0:T(2,128)} %param.14) | copy-start | bytes 3076
  0.0 65.2 %copy-start.6 = (f32[2,128]{1,0:T(2,128)S(1)}, f32[2,128]{1,0:T(2,128)}, u32[]{:S(2)}) copy-start(f32[2,128]{1,0:T(2,128)} %param.13) | copy-start | bytes 3076
  3.9 61.9 %copy-start.1 = (bf16[32,3072]{1,0:T(8,128)(2,1)S(1)}, bf16[32,3072]{1,0:T(8,128)(2,1)}, u32[]{:S(2)}) copy-start(bf16[32,3072]{1,0:T(8,128)(2,1)} %param.11) | copy-start | bytes 589828
  4.6 66.4 %all-to-all-start.1 = ((s32[128,1,4]{2,1,0:T(1,128)}), s32[128,1,4]{2,1,0:T(1,128)S(1)}, u32[]{:S(2)}, u32[]{:S(2)}) async-start(s32[128,1,4]{2,1,0:T(1,128)} %bitcast.11), calls=%async_computation.1 | async-start | bytes 131072 | tf_op jit(solution)/shard_map/all_to_all | solution.py:111
  66.3 0.9 copy-start.2
  71.0 41.4 %all-to-all-start = ((bf16[128,4,1152]{2,1,0:T(4,128)(2,1)}), bf16[128,4,1152]{2,1,0:T(4,128)(2,1)S(1)}, u32[]{:S(2)}, u32[]{:S(2)}) async-start(bf16[128,4,1152]{2,1,0:T(4,128)(2,1)} %broadcast_select_fusion), calls=%async_computation | async-start | bytes 2359296 | tf_op jit(solution)/shard_map/all_to_all | solution.py:110
  118.7 9.9 %copy-start.3 = (bf16[32,2,3072]{2,1,0:T(2,128)(2,1)S(1)}, bf16[32,2,3072]{2,1,0:T(2,128)(2,1)}, u32[]{:S(2)}) copy-start(bf16[32,2,3072]{2,1,0:T(2,128)(2,1)} %param.15) | copy-start | bytes 1179652
  120.2 25.5 %all-to-all-start.2 = ((bf16[128,4,384]{2,1,0:T(4,128)(2,1)}), bf16[128,4,384]{2,1,0:T(4,128)(2,1)S(1)}, u32[]{:S(2)}, u32[]{:S(2)}) async-start(bf16[128,4,384]{2,1,0:T(4,128)(2,1)} %reshape.231), calls=%async_computation.2 | async-start | bytes 786432 | tf_op jit(solution)/shard_map/all_to_all | solution.py:127
  145.8 1.1 copy-start.4
where the time goes:
time: 148 us
  waiting for transfers between devices  47 us (32%)
  starting transfers between devices  44.9 us (30%)
  blocking collectives  29.5 us (20%)
  local copies, waits for them, and re-layouts  12.6 us (9%)
  other arithmetic  7.28 us (5%)
  matrix products  5.29 us (4%)
    all_to_all x1, waiting for transfers between devices, per_device(): lax.all_to_all(outgoing, SEQ, split_axis=0, concat_axis=0, tiled=True)  30.8 us
    all_to_all x1, starting transfers between devices, per_device(): lax.all_to_all(segment_out, SEQ, split_axis=0, concat_axis=0, tiled=True)  27.4 us
    unnamed x1, blocking collectives  22.4 us
    all_to_all x1, waiting for transfers between devices, per_device(): lax.all_to_all(returning, SEQ, split_axis=0, concat_axis=0, tiled=True)  16.1 us
    all_to_all x1, starting transfers between devices, per_device(): lax.all_to_all(outgoing, SEQ, split_axis=0, concat_axis=0, tiled=True)  8.93 us
    all_to_all x1, starting transfers between devices, per_device(): lax.all_to_all(returning, SEQ, split_axis=0, concat_axis=0, tiled=True)  8.53 us
    all_gather x1, blocking collectives, gather_in_order(): parts = lax.all_gather(parts, axes[k])  7.09 us
    sub x1, matrix products, attend(): weights = jnp.exp(scores - largest)  3.02 us
  transfers between devices with their start and end apart: 3, of which 2 were waited for; matrix products, arithmetic and copies ran while one was open for 7% of the time, Pallas kernels for 0%

commit v1 on v0

v1 whole, which is shorter than its diff:
```python
import functools
import math

import jax
import jax.numpy as jnp
from jax import lax
from jax.experimental import pallas as pl
from jax.experimental.pallas import tpu as pltpu
from jax.sharding import Mesh
from jax.sharding import PartitionSpec as P

HEAD_DIM = 128
LANES = 128
CORES = 2
EPSILON = 1e-06
MASKED = -1e30
Y, X, C = "seq_0", "seq_1", "seq_2"
GROUPS_SEQ = ("groups", Y, X, C)
MESH = pl.DeviceIdType.MESH
F32 = jnp.float32
BF16 = jnp.bfloat16


def kernel(
    ny, nx, tok,
    hidden_hbm, query_hbm, key_hbm, value_hbm, query_gain, key_gain, gate_hbm, seg_ref, text_ref,
    out_ref,
    hid, que, key, val, gat,
    kra, qra, krb, qrb, ka, va, kb, vb, qa, qb,
    segrow, segall, turned, cola, colb, stra, gates,
    ma, la, acca, mb, lb, accb, oa, ob, atta, attb,
    load_sem, seg_send, seg_recv, all_send, all_recv,
    a_send, a_recv, b_send, b_recv, ra_send, ra_recv, rb_send, rb_recv, d_send, d_recv,
    oa_send, oa_recv, ob_send, ob_recv,
):
    ha = nx * CORES
    row_tok = ha * tok
    per_row = LANES // tok
    lane_rows = row_tok // LANES
    y, x, c = lax.axis_index(Y), lax.axis_index(X), lax.axis_index(C)
    idx = x * CORES + c

    def row_peer(i):
        return lax.rem(idx + i, ha)

    def row_dev(j):
        return {Y: y, X: j // CORES, C: lax.rem(j, CORES)}

    def col_dev(j):
        return {Y: j, X: x, C: c}

    def around(a, n):
        return lax.rem(a + 2 * n, n)

    partner = {Y: y, X: x, C: 1 - c}

    barrier = pltpu.get_barrier_semaphore()

    @pl.loop(1, ha)
    def _(i):
        pl.semaphore_signal(barrier, inc=1, device_id=row_dev(row_peer(i)), device_id_type=MESH)

    @pl.loop(1, ny)
    def _(j):
        pl.semaphore_signal(barrier, inc=1, device_id=col_dev(lax.rem(y + j, ny)), device_id_type=MESH)

    loads = [
        pltpu.make_async_copy(src, dst, load_sem.at[n])
        for n, (src, dst) in enumerate(
            [(key_hbm, key), (value_hbm, val), (query_hbm, que), (hidden_hbm, hid), (gate_hbm, gat)]
        )
    ]
    for load in loads:
        load.start()
    segrow[pl.ds(idx, 1)] = seg_ref[...].reshape(1, 1, LANES)
    for load in loads[:3]:
        load.wait()
    pl.semaphore_wait(barrier, ha - 1 + ny - 1)

    def remote(src, dst, send, recv, dev):
        return pltpu.make_async_remote_copy(
            src_ref=src, dst_ref=dst, send_sem=send, recv_sem=recv, device_id=dev, device_id_type=MESH
        )

    def head(ref, h):
        return ref.at[:, pl.ds(pl.multiple_of(h * HEAD_DIM, HEAD_DIM), HEAD_DIM)]

    def head_value(ref, h):
        return ref[:, pl.ds(pl.multiple_of(h * HEAD_DIM, HEAD_DIM), HEAD_DIM)]

    def seg_copy(i, src_idx, dst_idx):
        return remote(
            segrow.at[src_idx], segrow.at[src_idx], seg_send.at[i], seg_recv.at[i], row_dev(dst_idx)
        )

    @pl.loop(1, ha)
    def _(i):
        seg_copy(i, idx, row_peer(i)).start()

    tensors = (key, val, que)

    def a_target(n, slot):
        return (kra.at[slot], va.at[y, slot], qra.at[slot])[n]

    def b_target(n, slot):
        return (krb.at[slot], vb.at[slot, idx], qrb.at[slot])[n]

    def a_copy(n, i, src_idx, dst_idx):
        return remote(
            head(tensors[n], dst_idx), a_target(n, src_idx), a_send.at[n, i], a_recv.at[n, i], row_dev(dst_idx)
        )

    def b_copy(n, j, src_y, dst_y):
        return remote(
            head(tensors[n], ha + dst_y), b_target(n, src_y), b_send.at[n, j], b_recv.at[n, j], col_dev(dst_y)
        )

    for n in range(3):

        @pl.loop(1, ha)
        def _(i):
            a_copy(n, i, idx, row_peer(i)).start()

        @pl.loop(1, ny)
        def _(j):
            b_copy(n, j, y, lax.rem(y + j, ny)).start()

    kra[pl.ds(idx, 1)] = head_value(key, idx)[None]
    qra[pl.ds(idx, 1)] = head_value(que, idx)[None]
    va[pl.ds(y, 1), pl.ds(idx, 1)] = head_value(val, idx)[None, None]
    krb[pl.ds(y, 1)] = head_value(key, ha + y)[None]
    qrb[pl.ds(y, 1)] = head_value(que, ha + y)[None]
    vb[pl.ds(y, 1), pl.ds(idx, 1)] = head_value(val, ha + y)[None, None]

    def a_wait(n):
        @pl.loop(1, ha)
        def _(i):
            a_copy(n, i, lax.rem(idx + ha - i, ha), idx).wait_recv()

    def b_wait(n):
        @pl.loop(1, ny)
        def _(j):
            b_copy(n, j, lax.rem(y + ny - j, ny), y).wait_recv()

    @pl.loop(1, ha)
    def _(i):
        seg_copy(i, lax.rem(idx + ha - i, ha), idx).wait_recv()

    lane = lax.broadcasted_iota(jnp.int32, (1, LANES), 1)
    for r in range(lane_rows):
        joined = segrow[per_row * r]
        for g in range(1, per_row):
            joined = jnp.where(lane >= g * tok, segrow[per_row * r + g], joined)
        segall[pl.ds(y, 1), r : r + 1, :] = joined[None]

    def all_copy(j, src_y, dst_y):
        return remote(segall.at[src_y], segall.at[src_y], all_send.at[j], all_recv.at[j], col_dev(dst_y))

    @pl.loop(1, ny)
    def _(j):
        all_copy(j, y, lax.rem(y + j, ny)).start()

    def turn(row):
        return jnp.broadcast_to(row, (LANES, LANES)).T

    for r in range(lane_rows):
        cola[r * LANES : (r + 1) * LANES, :] = turn(segall[pl.ds(y, 1), r : r + 1, :].reshape(1, LANES))

    @pl.loop(1, ny)
    def _(j):
        all_copy(j, lax.rem(y + ny - j, ny), y).wait_recv()

    my_row, my_part = idx // per_row, lax.rem(idx, per_row)
    for yy in range(ny):
        turned[...] = turn(segall[yy, pl.ds(my_row, 1), :])
        colb[yy * tok : (yy + 1) * tok, :] = turned[pl.ds(pl.multiple_of(my_part * tok, tok), tok), :]

    def stream_of(col, order):
        rows = col.shape[0]

        def add(yy, count):
            for r in range(lane_rows):
                other = segall[yy, r : r + 1, :]
                place = yy * row_tok + r * LANES + lane
                count = count + jnp.where((col == other) & (place < order), 1.0, 0.0)
            return count

        count = lax.fori_loop(0, ny, add, jnp.zeros((rows, LANES), F32))
        position = jnp.sum(count, axis=1, keepdims=True)
        limit = jnp.sum(jnp.where(col == lane.astype(F32), text_ref[...], 0.0), axis=1, keepdims=True)
        return jnp.where(position >= limit, 1.0, 0.0)

    def normed(rows_in, gains, stream):
        wide = rows_in.astype(F32)
        inverse = lax.rsqrt(jnp.mean(wide * wide, axis=1, keepdims=True) + EPSILON)
        gain_rows = jnp.where(stream == 0.0, gains[0:1, :], gains[1:2, :])
        return (wide * inverse * gain_rows).astype(BF16)

    a_wait(0)
    for r in range(lane_rows):
        rows = pl.ds(r * LANES, LANES)
        slots = pl.ds(r * per_row, per_row)
        order = y * row_tok + r * LANES + lax.broadcasted_iota(jnp.int32, (LANES, LANES), 0)
        stream = stream_of(cola[rows, :], order)
        stra[rows, :] = jnp.broadcast_to(stream, (LANES, LANES))
        fresh = normed(kra[slots].reshape(LANES, HEAD_DIM), key_gain, stream)
        ka[pl.ds(y, 1), slots] = fresh.reshape(1, per_row, tok, HEAD_DIM)

    full = ny // 2 - 1
    full_x = nx // 2 - 1

    def a_part(buf, slot, way, whole):
        if whole:
            return buf.at[slot]
        return buf.at[slot, pl.ds(way * (ha // 2), ha // 2)]

    def b_part(buf, slot, way, whole):
        if whole:
            return buf.at[:, slot]
        return buf.at[pl.ds(way * (ny // 2), ny // 2), slot]

    def a_ring(t, way, s, arriving):
        buf = (ka, va)[t]
        sign = 1 if way == 0 else -1
        back = s + 1 if arriving else s
        part = a_part(buf, around(y - sign * back, ny), way, s < full)
        return remote(
            part, part, ra_send.at[t, way, s], ra_recv.at[t, way, s], col_dev(around(y + sign, ny))
        )

    def b_ring(t, way, s, arriving):
        buf = (kb, vb)[t]
        sign = 1 if way == 0 else -1
        back = s + 1 if arriving else s
        slot = around(x - sign * back, nx) * CORES + c
        part = b_part(buf, slot, way, s < full_x)
        dev = {Y: y, X: around(x + sign, nx), C: c}
        return remote(part, part, rb_send.at[t, way, s], rb_recv.at[t, way, s], dev)

    def d_copy(t, way, s, core):
        buf = (kb, vb)[t]
        sign = 1 if way == 0 else -1
        if s < 0:
            part = buf.at[:, x * CORES + core]
        else:
            slot = around(x - sign * (s + 1), nx) * CORES + core
            part = b_part(buf, slot, way, s < full_x)
        n = 0 if s < 0 else 1 + 2 * s + way
        return remote(part, part, d_send.at[t, n], d_recv.at[t, n], partner)

    ways = (0, 1)
    for way in ways:
        a_ring(0, way, 0, False).start()

    b_wait(0)
    order_b = lax.broadcasted_iota(jnp.int32, (ny * tok, LANES), 0)
    order_b = order_b // tok * row_tok + idx * tok + lax.rem(order_b, tok)
    stream_b = stream_of(colb[...], order_b)
    kb[:, pl.ds(idx, 1)] = normed(krb[...].reshape(ny * tok, HEAD_DIM), key_gain, stream_b).reshape(
        ny, 1, tok, HEAD_DIM
    )
    for way in ways:
        b_ring(0, way, 0, False).start()
    d_copy(0, 0, -1, c).start()

    a_wait(1)
    for way in ways:
        a_ring(1, way, 0, False).start()
    b_wait(1)
    for way in ways:
        b_ring(1, way, 0, False).start()
    d_copy(1, 0, -1, c).start()

    a_wait(2)
    for r in range(lane_rows):
        rows = pl.ds(r * LANES, LANES)
        slots = pl.ds(r * per_row, per_row)
        qa[rows, :] = normed(qra[slots].reshape(LANES, HEAD_DIM), query_gain, stra[rows, 0:1])
    b_wait(2)
    qb[...] = normed(qrb[...].reshape(ny * tok, HEAD_DIM), query_gain, stream_b)

    for m, l, acc in ((ma, la, acca), (mb, lb, accb)):
        m[...] = jnp.full(m.shape, MASKED, F32)
        l[...] = jnp.zeros(l.shape, F32)
        acc[...] = jnp.zeros(acc.shape, F32)

    scale = 1.0 / math.sqrt(HEAD_DIM)

    def attend(q, cols, m, l, acc, keys, vals, slot):
        block = LANES

        @pl.loop(0, q.shape[0] // block)
        def _(b):
            rows = pl.ds(pl.multiple_of(b * block, block), block)
            kk = keys[slot].reshape(row_tok, HEAD_DIM)
            vv = vals[slot].reshape(row_tok, HEAD_DIM)
            s = lax.dot_general(q[rows, :], kk, (((1,), (1,)), ((), ())), preferred_element_type=F32) * scale
            mine = cols[rows, :]
            parts = []
            for r in range(lane_rows):
                other = segall[slot, r : r + 1, :]
                parts.append(jnp.where(mine == other, s[:, r * LANES : (r + 1) * LANES], MASKED))
            top = parts[0]
            for part in parts[1:]:
                top = jnp.maximum(top, part)
            old = m[rows, :]
            new = jnp.maximum(old, jnp.max(top, axis=1, keepdims=True))
            shrink = jnp.exp(old - new)
            parts = [jnp.exp(part - new) for part in parts]
            total = parts[0]
            for part in parts[1:]:
                total = total + part
            m[rows, :] = new
            l[rows, :] = l[rows, :] * shrink + total
            weights = jnp.concatenate([part.astype(BF16) for part in parts], axis=1)
            acc[rows, :] = acc[rows, :] * shrink + jnp.dot(weights, vv, preferred_element_type=F32)

    def attend_a(slot):
        attend(qa, cola, ma, la, acca, ka, va, slot)

    attend_a(y)

    for load in loads[3:]:
        load.wait()
    own = pl.ds(pl.multiple_of(idx * tok, tok), tok)
    entry = cola[own, :] * 2.0 + stra[own, :]
    pick = jnp.where(entry == lane.astype(F32), 1.0, 0.0).astype(BF16)[:, : gat.shape[0]]
    gates[...] = jnp.dot(pick, gat[...], preferred_element_type=F32)

    steps = max(full, full_x) + 1
    for s in range(steps):
        in_a, in_b = s <= full, s <= full_x
        for t in (0, 1):
            if in_b:
                for way in ways:
                    b_ring(t, way, s, True).wait_recv()
                    if s < full_x:
                        b_ring(t, way, s + 1, False).start()
                    d_copy(t, way, s, c).start()
            if in_a and s < full:
                for way in ways:
                    a_ring(t, way, s, True).wait_recv()
                    a_ring(t, way, s + 1, False).start()
        if s < full:
            attend_a(around(y - s - 1, ny))
            attend_a(around(y + s + 1, ny))

    for t in (0, 1):
        d_copy(t, 0, -1, 1 - c).wait_recv()
        for s in range(full_x + 1):
            for way in ways:
                d_copy(t, way, s, 1 - c).wait_recv()

    @pl.loop(0, ny)
    def _(slot):
        attend(qb, colb, mb, lb, accb, kb, vb, slot)

    def finish(l, acc):
        return (acc[...] / jnp.sum(l[...], axis=1, keepdims=True)).astype(BF16)

    ob[...] = finish(lb, accb).reshape(ny, tok, HEAD_DIM)

    def ob_copy(j, src_y, dst_y):
        return remote(ob.at[dst_y], attb.at[src_y], ob_send.at[j], ob_recv.at[j], col_dev(dst_y))

    @pl.loop(1, ny)
    def _(j):
        ob_copy(j, y, lax.rem(y + j, ny)).start()

    attb[pl.ds(y, 1)] = ob[pl.ds(y, 1)]

    for t in (0, 1):
        for way in ways:
            a_ring(t, way, full, True).wait_recv()
    attend_a(around(y + ny // 2, ny))
    oa[...] = finish(la, acca).reshape(ha, tok, HEAD_DIM)

    def oa_copy(i, src_idx, dst_idx):
        return remote(oa.at[dst_idx], atta.at[src_idx], oa_send.at[i], oa_recv.at[i], row_dev(dst_idx))

    @pl.loop(1, ha)
    def _(i):
        oa_copy(i, idx, row_peer(i)).start()

    atta[pl.ds(idx, 1)] = oa[pl.ds(idx, 1)]

    @pl.loop(1, ha)
    def _(i):
        seg_copy(i, idx, row_peer(i)).wait_send()
        for n in range(3):
            a_copy(n, i, idx, row_peer(i)).wait_send()

    @pl.loop(1, ny)
    def _(j):
        all_copy(j, y, lax.rem(y + j, ny)).wait_send()
        for n in range(3):
            b_copy(n, j, y, lax.rem(y + j, ny)).wait_send()

    for t in (0, 1):
        d_copy(t, 0, -1, c).wait_send()
        for way in ways:
            for s in range(full + 1):
                a_ring(t, way, s, False).wait_send()
            for s in range(full_x + 1):
                b_ring(t, way, s, False).wait_send()
                d_copy(t, way, s, c).wait_send()

    @pl.loop(1, ny)
    def _(j):
        ob_copy(j, lax.rem(y + ny - j, ny), y).wait_recv()

    @pl.loop(1, ha)
    def _(i):
        oa_copy(i, lax.rem(idx + ha - i, ha), idx).wait_recv()

    for h in range(ha + ny):
        columns = slice(h * HEAD_DIM, (h + 1) * HEAD_DIM)
        result = atta[h] if h < ha else attb[h - ha]
        out_ref[:, columns] = (
            hid[:, columns].astype(F32) + gates[:, columns] * result.astype(F32)
        ).astype(BF16)

    @pl.loop(1, ny)
    def _(j):
        ob_copy(j, y, lax.rem(y + j, ny)).wait_send()

    @pl.loop(1, ha)
    def _(i):
        oa_copy(i, idx, row_peer(i)).wait_send()


def per_device(
    ny, nx, hidden, queries, key_rows, values, query_gain, key_gain, gate_table, segment, text_count
):
    tok, width = hidden.shape
    requests = text_count.shape[0]
    ha = nx * CORES
    row_tok = ha * tok
    seg_row = jnp.tile(segment, LANES // tok)[None, :].astype(F32)
    text_row = jnp.pad(text_count, (0, LANES - requests))[None, :].astype(F32)
    gate_rows = gate_table.reshape(2 * requests, width)
    anywhere = pl.BlockSpec(memory_space=pl.ANY)
    vmem = pl.BlockSpec(memory_space=pltpu.VMEM)
    dma = pltpu.SemaphoreType.DMA
    heads = (tok, HEAD_DIM)
    half_y, half_x = ny // 2, nx // 2
    return pl.pallas_call(
        functools.partial(kernel, ny, nx, tok),
        out_shape=jax.ShapeDtypeStruct((tok, width), BF16),
        in_specs=[anywhere] * 4 + [vmem] * 2 + [anywhere] + [vmem] * 2,
        out_specs=vmem,
        scratch_shapes=[
            pltpu.VMEM((tok, width), BF16),
            pltpu.VMEM((tok, width), BF16),
            pltpu.VMEM((tok, width), BF16),
            pltpu.VMEM((tok, width), BF16),
            pltpu.VMEM((2 * requests, width), BF16),
            pltpu.VMEM((ha, *heads), BF16),
            pltpu.VMEM((ha, *heads), BF16),
            pltpu.VMEM((ny, *heads), BF16),
            pltpu.VMEM((ny, *heads), BF16),
            pltpu.VMEM((ny, ha, *heads), BF16),
            pltpu.VMEM((ny, ha, *heads), BF16),
            pltpu.VMEM((ny, ha, *heads), BF16),
            pltpu.VMEM((ny, ha, *heads), BF16),
            pltpu.VMEM((row_tok, HEAD_DIM), BF16),
            pltpu.VMEM((ny * tok, HEAD_DIM), BF16),
            pltpu.VMEM((ha, 1, LANES), F32),
            pltpu.VMEM((ny, 8, LANES), F32),
            pltpu.VMEM((LANES, LANES), F32),
            pltpu.VMEM((row_tok, LANES), F32),
            pltpu.VMEM((ny * tok, LANES), F32),
            pltpu.VMEM((row_tok, LANES), F32),
            pltpu.VMEM((tok, width), F32),
            pltpu.VMEM((row_tok, LANES), F32),
            pltpu.VMEM((row_tok, LANES), F32),
            pltpu.VMEM((row_tok, HEAD_DIM), F32),
            pltpu.VMEM((ny * tok, LANES), F32),
            pltpu.VMEM((ny * tok, LANES), F32),
            pltpu.VMEM((ny * tok, HEAD_DIM), F32),
            pltpu.VMEM((ha, *heads), BF16),
            pltpu.VMEM((ny, *heads), BF16),
            pltpu.VMEM((ha, *heads), BF16),
            pltpu.VMEM((ny, *heads), BF16),
            dma((5,)),
            dma((ha,)),
            dma((ha,)),
            dma((ny,)),
            dma((ny,)),
            dma((3, ha)),
            dma((3, ha)),
            dma((3, ny)),
            dma((3, ny)),
            dma((2, 2, half_y)),
            dma((2, 2, half_y)),
            dma((2, 2, half_x)),
            dma((2, 2, half_x)),
            dma((2, 1 + 2 * half_x)),
            dma((2, 1 + 2 * half_x)),
            dma((ha,)),
            dma((ha,)),
            dma((ny,)),
            dma((ny,)),
        ],
        compiler_params=pltpu.CompilerParams(
            collective_id=0, has_side_effects=True, vmem_limit_bytes=40 * 1024 * 1024
        ),
        name="joint_attention",
    )(hidden, queries, key_rows, values, query_gain, key_gain, gate_rows, seg_row, text_row)


def solution(mesh):
    groups, seq = mesh.shape["groups"], mesh.shape["seq"]
    nx = math.isqrt(seq // CORES)
    ny = seq // CORES // nx
    finer = Mesh(mesh.devices.reshape(groups, ny, nx, CORES), GROUPS_SEQ)
    placed = (
        P(GROUPS_SEQ, None),
        P(GROUPS_SEQ, None),
        P(GROUPS_SEQ, None),
        P(GROUPS_SEQ, None),
        P(),
        P(),
        P("groups", None, None),
        P(GROUPS_SEQ),
        P("groups"),
    )
    return jax.shard_map(
        functools.partial(per_device, ny, nx),
        mesh=finer,
        in_specs=placed,
        out_specs=P(GROUPS_SEQ, None),
        check_vma=False,
    )
```

time: 148 us -> 80.9 us (0.55)
  Pallas kernels: 0 us -> 77.9 us
  waiting for transfers between devices: 47 us -> 0 us
  starting transfers between devices: 44.9 us -> 0 us
  blocking collectives: 29.5 us -> 0 us
  local copies, waits for them, and re-layouts: 12.6 us -> 2.06 us
  other arithmetic: 7.28 us -> 0.7 us
  matrix products: 5.29 us -> 0 us
    pallas_call x0 -> x1, Pallas kernels: none -> 77.9 us  [per_device(): pl.pallas_call(functools.partial(kernel, ny, nx, tok), out_shape=jax.Shap...]
    all_to_all x3 -> x0, waiting for transfers between devices: 47 us -> none  [the longest x1 30.8 us: per_device(): lax.all_to_all(outgoing, SEQ, split_axis=0, concat_axis=0, tiled=True)]
    all_to_all x3 -> x0, starting transfers between devices: 44.9 us -> none  [the longest x1 27.4 us: per_device(): lax.all_to_all(segment_out, SEQ, split_axis=0, concat_axis=0, tiled=True)]
    unnamed x1 -> x0, blocking collectives: 22.4 us -> none
    all_gather x1 -> x0, blocking collectives: 7.09 us -> none  [gather_in_order(): parts = lax.all_gather(parts, axes[k])]
    gather x6 -> x0, local copies, waits for them, and re-layouts: 3.92 us -> none  [the longest x1 1.43 us: per_device(): jnp.take(segment, bucket_index, axis=0, mode='fill', fill_value=-1)]
    sub x1 -> x0, matrix products: 3.02 us -> none  [attend(): weights = jnp.exp(scores - largest)]
    select_n x5 -> x0, other arithmetic: 2.44 us -> none  [the longest x2 1.65 us: per_device(): jnp.take(stacked, bucket_index, axis=1, mode='fill', fill_value=0)]
  transfers between devices with their start and end apart: 3 -> 0, of which waited for: 2 -> 0; matrix products, arithmetic and copies ran while one was open for 7% -> 0% of each run, Pallas kernels for 0% -> 0%
where the time goes in v1:
time: 80.9 us; the launch traced here: 80.8 us
  Pallas kernels  77.9 us (96%)
  local copies, waits for them, and re-layouts  2.06 us (3%)
    pallas_call x1, Pallas kernels, per_device(): pl.pallas_call(functools.partial(kernel, ny, nx, tok), out_shape=jax.Shap...  77.9 us

profile of v1, /device:TPU:513, one launch (start us, length us, event | category | flops | bytes accessed | tf_op | source)
XLA Modules:
  0.0 80.8 jit_solution(6875736120294152477)
XLA Ops:
  0.0 0.0 copy-start.6
  0.0 0.0 copy-start.4
  0.0 0.0 copy-start.5
  0.0 0.7 convert_element_type.10
  0.7 0.0 copy-done.6
  0.7 0.1 convert_element_type.11.seg_ref
  0.8 0.0 copy-start
  0.8 0.0 copy-start.1
  0.8 0.0 copy-start.2
  0.8 0.0 copy-start.3
  0.8 1.2 %reshape.18.gate_hbm = bf16[64,3072]{1,0:T(8,128)(2,1)S(1)} reshape(bf16[32,2,3072]{2,1,0:T(2,128)(2,1)} %param.15) | data formatting | bytes 786432 | tf_op jit(solution)/shard_map/reshape | solution.py:441
  2.0 0.0 copy-done.4
  2.0 0.0 copy-done.5
  2.1 0.0 copy-done
  2.1 0.0 copy-done.1
  2.1 0.0 copy-done.2
  2.1 0.0 copy-done.3
  2.1 77.9 %joint_attention.1 = bf16[32,3072]{1,0:T(8,128)(2,1)S(1)} custom-call(bf16[32,3072]{1,0:T(8,128)(2,1)S(1)} %copy-done, bf16[32,3072]{1,0:T(8,128)(2,1)S(1)} %copy-done.1, bf16[32,3072]{1,0:T(8,128)(2,1)S(1)} %copy-done.2, bf16[32,3072]{1,0:T(8,128)(2,1)S(1)} %copy-done.3, f32[2,128]{1,0:T(2,128)S(1)} %copy-done.4, f32[2,128]{1,0:T(2,128)S(1)} %copy-done.5, ...), custom_call_target="tpu_custom_call" | custom-call | tf_op jit(solution)/shard_map/joint_attention/pallas_call | solution.py:447
  80.1 0.7 copy.11
  (2 shorter events, 0.0 us)
Async XLA Ops:
  0.0 0.7 copy-start.6
  0.0 2.0 %copy-start.4 = (f32[2,128]{1,0:T(2,128)S(1)}, f32[2,128]{1,0:T(2,128)}, u32[]{:S(2)}) copy-start(f32[2,128]{1,0:T(2,128)} %query_gain.1) | copy-start | bytes 3076
  0.0 2.0 %copy-start.5 = (f32[2,128]{1,0:T(2,128)S(1)}, f32[2,128]{1,0:T(2,128)}, u32[]{:S(2)}) copy-start(f32[2,128]{1,0:T(2,128)} %key_gain.1) | copy-start | bytes 3076
  0.8 1.3 %copy-start = (bf16[32,3072]{1,0:T(8,128)(2,1)S(1)}, bf16[32,3072]{1,0:T(8,128)(2,1)}, u32[]{:S(2)}) copy-start(bf16[32,3072]{1,0:T(8,128)(2,1)} %hidden_hbm.1) | copy-start | bytes 589828
  0.8 1.3 %copy-start.1 = (bf16[32,3072]{1,0:T(8,128)(2,1)S(1)}, bf16[32,3072]{1,0:T(8,128)(2,1)}, u32[]{:S(2)}) copy-start(bf16[32,3072]{1,0:T(8,128)(2,1)} %query_hbm.1) | copy-start | bytes 589828
  0.8 1.3 %copy-start.2 = (bf16[32,3072]{1,0:T(8,128)(2,1)S(1)}, bf16[32,3072]{1,0:T(8,128)(2,1)}, u32[]{:S(2)}) copy-start(bf16[32,3072]{1,0:T(8,128)(2,1)} %key_hbm.1) | copy-start | bytes 589828
  0.8 1.3 %copy-start.3 = (bf16[32,3072]{1,0:T(8,128)(2,1)S(1)}, bf16[32,3072]{1,0:T(8,128)(2,1)}, u32[]{:S(2)}) copy-start(bf16[32,3072]{1,0:T(8,128)(2,1)} %value_hbm.1) | copy-start | bytes 589828

commit v2 on v0

v2 whole, which is shorter than its diff:
```python
import functools
import math

import jax
import jax.numpy as jnp
from jax import lax
from jax.experimental import pallas as pl
from jax.experimental.pallas import tpu as pltpu
from jax.sharding import Mesh
from jax.sharding import PartitionSpec as P

HEAD_DIM = 128
LANES = 128
CORES = 2
EPSILON = 1e-06
LOWEST = -1e30
SAME = (128.0, 64.0)
LATER = 64.0
BLOCK = 256
VMEM_BYTES = 60 * 1024 * 1024
Y, X, C = "seq_0", "seq_1", "seq_2"
GROUPS_SEQ = ("groups", Y, X, C)
MESH = pl.DeviceIdType.MESH
F32 = jnp.float32
BF16 = jnp.bfloat16


def kernel(
    ny, nx, tok, requests,
    hidden_hbm, query_hbm, key_hbm, value_hbm, query_gain, key_gain, gate_hbm, seg_ref, text_ref,
    out_ref,
    hid, que, key, val, gat,
    kra, qra, krb, qrb, ka, va, kb, vb, qa, qb,
    segrow, segall, codea, codeb, tri, hot, cola, gains, gates, kwork, held,
    ma, la, acca, mb, lb, accb, oa, ob, atta, attb,
    load_sem, seg_send, seg_recv, all_send, all_recv,
    a_send, a_recv, b_send, b_recv, ra_send, ra_recv, rb_send, rb_recv, d_send, d_recv,
    oa_send, oa_recv, ob_send, ob_recv,
):
    ha = nx * CORES
    row_tok, col_tok = ha * tok, ny * tok
    per = LANES // tok
    a_rows, b_rows = row_tok // LANES, col_tok // LANES
    y, x, c = lax.axis_index(Y), lax.axis_index(X), lax.axis_index(C)
    idx = x * CORES + c
    ways = (0, 1)

    loads = [
        pltpu.make_async_copy(src, dst, load_sem.at[n])
        for n, (src, dst) in enumerate(
            [(key_hbm, key), (value_hbm, val), (query_hbm, que), (hidden_hbm, hid), (gate_hbm, gat)]
        )
    ]
    for load in loads:
        load.start()

    def around(a, n):
        return lax.rem(a + 2 * n, n)

    row = []
    for dx in range(nx):
        for dc in range(CORES):
            if dx or dc:
                xx = around(x + dx, nx)
                cc = c if dc == 0 else 1 - c
                row.append((xx * CORES + cc, {Y: y, X: xx, C: cc}))
    col = []
    for dy in range(1, ny):
        yy = around(y + dy, ny)
        col.append((yy, {Y: yy, X: x, C: c}))
    partner = {Y: y, X: x, C: 1 - c}

    barrier = pltpu.get_barrier_semaphore()
    for _, dev in row + col:
        pl.semaphore_signal(barrier, inc=1, device_id=dev, device_id_type=MESH)

    lane = lax.broadcasted_iota(jnp.int32, (1, LANES), 1)
    lane_f = lane.astype(F32)
    place = lax.rem(lane, tok)
    mine = jnp.zeros((1, LANES), F32)
    for i in range(tok):
        mine = jnp.where(place == i, seg_ref[i].astype(F32), mine)
    segrow[pl.ds(idx, 1)] = mine.reshape(1, 1, LANES)
    down = lax.broadcasted_iota(jnp.int32, (requests, LANES), 0)
    limit = jnp.zeros((requests, LANES), F32)
    for i in range(requests):
        limit = jnp.where(down == i, text_ref[i].astype(F32), limit)
    down = down.astype(F32)
    deep = lax.broadcasted_iota(jnp.int32, (LANES, LANES), 0).astype(F32)
    for r in range(a_rows):
        first = lax.broadcasted_iota(jnp.int32, (LANES, row_tok), 0) + r * LANES
        second = lax.broadcasted_iota(jnp.int32, (LANES, row_tok), 1)
        tri[r * LANES : (r + 1) * LANES, :] = jnp.where(first < second, 1.0, 0.0).astype(BF16)

    def turn(line):
        return jnp.broadcast_to(line, (LANES, LANES)).T

    for i in range(2):
        gains[i] = turn(key_gain[i : i + 1, :])
    for m, l, acc in ((ma, la, acca), (mb, lb, accb)):
        m[...] = jnp.full(m.shape, LOWEST, F32)
        l[...] = jnp.zeros(l.shape, F32)
        acc[...] = jnp.zeros(acc.shape, F32)

    loads[0].wait()
    pl.semaphore_wait(barrier, len(row) + len(col))

    def remote(src, dst, send, recv, dev):
        return pltpu.make_async_remote_copy(
            src_ref=src, dst_ref=dst, send_sem=send, recv_sem=recv, device_id=dev, device_id_type=MESH
        )

    def head(ref, h):
        return ref.at[:, pl.ds(pl.multiple_of(h * HEAD_DIM, HEAD_DIM), HEAD_DIM)]

    def head_value(ref, h):
        return ref[:, pl.ds(pl.multiple_of(h * HEAD_DIM, HEAD_DIM), HEAD_DIM)]

    def wait_all(ref, sem):
        pltpu.make_async_copy(ref, ref, sem).wait()

    tensors = (key, val, que)
    a_in = (kra, va.at[y], qra)
    b_in = (krb, vb.at[idx], qrb)

    def a_start(n):
        for j, dev in row:
            remote(head(tensors[n], j), a_in[n].at[idx], a_send.at[n], a_recv.at[n], dev).start()

    def b_start(n):
        for j, dev in col:
            remote(head(tensors[n], ha + j), b_in[n].at[y], b_send.at[n], b_recv.at[n], dev).start()

    a_start(0)
    for _, dev in row:
        remote(segrow.at[idx], segrow.at[idx], seg_send, seg_recv, dev).start()
    for n in range(3):
        if n:
            loads[n].wait()
        b_start(n)

    kra[pl.ds(idx, 1)] = head_value(key, idx)[None]
    qra[pl.ds(idx, 1)] = head_value(que, idx)[None]
    va[pl.ds(y, 1), pl.ds(idx, 1)] = head_value(val, idx)[None, None]
    krb[pl.ds(y, 1)] = head_value(key, ha + y)[None]
    qrb[pl.ds(y, 1)] = head_value(que, ha + y)[None]
    vb[pl.ds(idx, 1), pl.ds(y, 1)] = head_value(val, ha + y)[None, None]

    full, full_x = ny // 2 - 1, nx // 2 - 1

    def half(ref, t, way, count):
        if t == 0:
            return ref.at[:, pl.ds(way * (HEAD_DIM // 2), HEAD_DIM // 2)]
        return ref.at[pl.ds(way * (count // 2), count // 2)]

    def a_part(t, slot, way, s):
        part = (ka, va)[t].at[slot]
        return part if s < full else half(part, t, way, ha)

    def b_part(t, slot, way, s):
        part = (kb, vb)[t].at[slot]
        return part if s < full_x else half(part, t, way, ny)

    def a_ring(t, way, s, back):
        sign = 1 - 2 * way
        part = a_part(t, around(y - sign * back, ny), way, s)
        dev = {Y: around(y + sign, ny), X: x, C: c}
        return remote(part, part, ra_send.at[t], ra_recv.at[t, way, s], dev)

    def b_ring(t, way, s, back):
        sign = 1 - 2 * way
        part = b_part(t, around(x - sign * back, nx) * CORES + c, way, s)
        dev = {Y: y, X: around(x + sign, nx), C: c}
        return remote(part, part, rb_send.at[t], rb_recv.at[t, way, s], dev)

    def d_copy(t, way, s, core):
        if s < 0:
            part = (kb, vb)[t].at[x * CORES + core]
        else:
            sign = 1 - 2 * way
            part = b_part(t, around(x - sign * (s + 1), nx) * CORES + core, way, s)
        return remote(part, part, d_send.at[t], d_recv.at[t, 0 if s < 0 else 1 + 2 * s + way], partner)

    def turned(raw):
        return raw.reshape(LANES, HEAD_DIM).astype(F32).T.astype(BF16)

    peers_a, peers_b = pl.ds(0, ha - 1), pl.ds(0, ny - 1)

    def a_pass(t, s):
        for way in ways:
            a_ring(t, way, s, s + 1).wait_recv()
            if s < full:
                a_ring(t, way, s + 1, s + 1).start()

    def b_pass(t, s):
        for way in ways:
            b_ring(t, way, s, s + 1).wait_recv()
            if s < full_x:
                b_ring(t, way, s + 1, s + 1).start()
            d_copy(t, way, s, c).start()

    wait_all(kra.at[peers_a], a_send.at[0])
    a_start(1)
    wait_all(krb.at[peers_b], b_recv.at[0])
    for r in range(b_rows):
        kb[pl.ds(idx, 1), r : r + 1] = turned(krb[r * per : (r + 1) * per])[None, None]
    wait_all(kra.at[peers_a], a_recv.at[0])
    for r in range(a_rows):
        ka[pl.ds(y, 1), r : r + 1] = turned(kra[r * per : (r + 1) * per])[None, None]
    for way in ways:
        a_ring(0, way, 0, 0).start()
    wait_all(segrow.at[peers_a], seg_recv)
    for r in range(a_rows):
        joined = segrow[per * r]
        for g in range(1, per):
            joined = jnp.where(lane >= g * tok, segrow[per * r + g], joined)
        segall[pl.ds(y, 1), r : r + 1, :] = joined[None]
    for _, dev in col:
        remote(segall.at[y], segall.at[y], all_send, all_recv, dev).start()
    wait_all(kra.at[peers_a], a_send.at[1])
    for way in ways:
        b_ring(0, way, 0, 0).start()
    d_copy(0, 0, -1, c).start()
    wait_all(vb.at[0, peers_b], b_recv.at[1])
    for way in ways:
        b_ring(1, way, 0, 0).start()
    d_copy(1, 0, -1, c).start()
    a_start(2)
    wait_all(va.at[0, peers_a], a_recv.at[1])
    for way in ways:
        a_ring(1, way, 0, 0).start()
    a_pass(0, 0)
    wait_all(segall.at[peers_b], all_recv)
    for yy in range(ny):
        for r in range(a_rows):
            hot[yy * requests : (yy + 1) * requests, r * LANES : (r + 1) * LANES] = jnp.where(
                down == segall[yy, r : r + 1, :], 1.0, 0.0
            ).astype(BF16)
    base = -limit
    for yy in range(ny):
        own = hot[yy * requests : (yy + 1) * requests, :]
        own_f = own.astype(F32)
        before = jnp.dot(own, tri[...], preferred_element_type=F32)
        for r in range(a_rows):
            part = slice(r * LANES, (r + 1) * LANES)
            over = jnp.sum(own_f[:, part] * (before[:, part] + base), axis=0, keepdims=True)
            codea[yy, r : r + 1, :] = segall[yy, r : r + 1, :] + jnp.where(over >= 0.0, LATER, 0.0)
        base = base + jnp.sum(own_f, axis=1, keepdims=True)
    for q in range(b_rows):
        for g in range(per):
            line = None
            for h in range(per):
                rows = codea[q * per + h]
                if h != g:
                    rows = pltpu.roll(rows, (h - g) * tok % LANES, 1)
                line = rows if line is None else jnp.where(lane >= h * tok, rows, line)
            codeb[q, g] = line

    def code_a(slot, r):
        return codea[slot, r : r + 1, :]

    def code_b(j, r):
        return codeb[r, lax.rem(j, per), pl.ds(j // per, 1), :]

    def query(raw, code):
        code = turn(code)
        late = code >= LATER
        wide = raw.reshape(LANES, HEAD_DIM).astype(F32)
        inverse = lax.rsqrt(jnp.mean(wide * wide, axis=1, keepdims=True) + EPSILON)
        fresh = wide * inverse * jnp.where(late, query_gain[1:2, :], query_gain[0:1, :])
        seg = jnp.where(late, code - LATER, code)
        same = jnp.where(seg == lane_f, SAME[0], 0.0)
        return jnp.concatenate([fresh.astype(BF16), same.astype(BF16)], axis=1), code

    rate = math.log2(math.e) / math.sqrt(HEAD_DIM)

    def key_work(blocks):
        for n, (raw, code) in enumerate(blocks):
            late = code >= LATER
            wide = raw.astype(F32)
            inverse = lax.rsqrt(jnp.sum(wide * wide, axis=0, keepdims=True) * (1.0 / HEAD_DIM) + EPSILON)
            fresh = wide * inverse * jnp.where(late, gains[1], gains[0])
            part = slice(n * LANES, (n + 1) * LANES)
            kwork[0:HEAD_DIM, part] = fresh.astype(BF16)
            seg = jnp.where(late, code - LATER, code)
            kwork[HEAD_DIM : 2 * HEAD_DIM, part] = jnp.where(deep == seg, SAME[1], 0.0).astype(BF16)
        return len(blocks)

    def soften(q, m, l, acc, count, rows):
        s = jnp.dot(q[rows, :], kwork[:, : count * LANES], preferred_element_type=F32)
        parts = [s[:, n * LANES : (n + 1) * LANES] for n in range(count)]
        top = functools.reduce(jnp.maximum, parts)
        old = m[rows, :]
        new = jnp.maximum(old, jnp.max(top, axis=1, keepdims=True))
        shrink = jnp.exp2((old - new) * rate)
        parts = [jnp.exp2((part - new) * rate) for part in parts]
        m[rows, :] = new
        l[rows, :] = l[rows, :] * shrink + functools.reduce(jnp.add, parts)
        weights = jnp.concatenate([part.astype(BF16) for part in parts], axis=1)
        return weights, acc[rows, :] * shrink

    def attend(q, m, l, acc, blocks, vals):
        count = key_work(blocks)
        step = min(BLOCK, q.shape[0])
        for b in range(q.shape[0] // step):
            rows = slice(b * step, (b + 1) * step)
            weights, kept = soften(q, m, l, acc, count, rows)
            acc[rows, :] = kept + jnp.dot(weights, vals, preferred_element_type=F32)

    def blocks_a(slots):
        return [(ka[slot, r], code_a(slot, r)) for slot in slots for r in range(a_rows)]

    def attend_a(slots):
        vals = jnp.concatenate([va[slot].reshape(row_tok, HEAD_DIM) for slot in slots], axis=0)
        attend(qa, ma, la, acca, blocks_a(slots), vals)

    def attend_b(places):
        ids = [place * CORES + core for place in places for core in range(CORES)]
        blocks = [(kb[j, r], code_b(j, r)) for j in ids for r in range(b_rows)]
        vals = jnp.concatenate([vb[j].reshape(col_tok, HEAD_DIM) for j in ids], axis=0)
        attend(qb, mb, lb, accb, blocks, vals)

    def finish(l, acc):
        return (acc / jnp.sum(l, axis=1, keepdims=True)).astype(BF16)

    def b_slots(s):
        for t in (0, 1):
            for way in ways if s >= 0 else (0,):
                d_copy(t, way, s, 1 - c).wait_recv()
        if s < 0:
            return [x]
        if s < full_x:
            return [around(x - s - 1, nx), around(x + s + 1, nx)]
        return [around(x + nx // 2, nx)]

    b_pass(0, 0)
    b_pass(1, 0)
    wait_all(qrb.at[peers_b], b_recv.at[2])
    wait_all(qra.at[peers_a], a_recv.at[2])
    for r in range(a_rows):
        part = slice(r * LANES, (r + 1) * LANES)
        qa[part, :], cola[part, :] = query(qra[r * per : (r + 1) * per], code_a(y, r))
    for r in range(b_rows):
        part = slice(r * LANES, (r + 1) * LANES)
        qb[part, :], _ = query(qrb[r * per : (r + 1) * per], code_b(idx, r))
    attend_a([y])
    a_pass(1, 0)
    attend_b(b_slots(-1))

    for load in loads[3:]:
        load.wait()
    code = cola[pl.ds(pl.multiple_of(idx * tok, tok), tok), :]
    late = code >= LATER
    seg = jnp.where(late, code - LATER, code)
    total = None
    for kind in range(2):
        pick = jnp.where((seg == lane_f) & (late == (kind == 1)), 1.0, 0.0).astype(BF16)[:, :requests]
        term = jnp.dot(pick, gat[:, kind, :], preferred_element_type=F32)
        total = term if total is None else total + term
    gates[...] = total

    b_step, b_done = 1, -1
    for s in range(full):
        if s + 1 < full:
            a_pass(0, s + 1)
        if b_step <= full_x:
            b_pass(0, b_step)
            b_pass(1, b_step)
            b_step += 1
        attend_a([around(y - s - 1, ny), around(y + s + 1, ny)])
        if s + 1 < full:
            a_pass(1, s + 1)
        if b_done + 1 < b_step:
            b_done += 1
            places = b_slots(b_done)
            attend_b(places)
    for s in range(b_step, full_x + 1):
        b_pass(0, s)
        b_pass(1, s)
    for s in range(b_done + 1, full_x + 1):
        places = b_slots(s)
        attend_b(places)

    ob[...] = finish(lb[...], accb[...]).reshape(ny, tok, HEAD_DIM)
    for j, dev in col:
        remote(ob.at[j], attb.at[y], ob_send, ob_recv, dev).start()
    attb[pl.ds(y, 1)] = ob[pl.ds(y, 1)]

    a_pass(0, full)
    last = around(y + ny // 2, ny)
    count = key_work(blocks_a([last]))
    for b in range(a_rows):
        rows = slice(b * LANES, (b + 1) * LANES)
        held[rows, :], acca[rows, :] = soften(qa, ma, la, acca, count, rows)
    a_pass(1, full)
    oa[...] = finish(
        la[...], acca[...] + jnp.dot(held[...], va[last].reshape(row_tok, HEAD_DIM), preferred_element_type=F32)
    ).reshape(ha, tok, HEAD_DIM)
    for j, dev in row:
        remote(oa.at[j], atta.at[idx], oa_send, oa_recv, dev).start()
    atta[pl.ds(idx, 1)] = oa[pl.ds(idx, 1)]

    wait_all(segrow.at[pl.ds(0, ha - 1)], seg_send)
    wait_all(segall.at[pl.ds(0, ny - 1)], all_send)
    wait_all(kra.at[peers_a], a_send.at[2])
    for n in range(3):
        wait_all(krb.at[peers_b], b_send.at[n])
    for t in (0, 1):
        wait_all((ka, va)[t].at[pl.ds(0, ny - 1)], ra_send.at[t])
        wait_all((kb, vb)[t].at[pl.ds(0, nx - 1)], rb_send.at[t])
        wait_all((kb, vb)[t].at[pl.ds(0, nx)], d_send.at[t])

    wait_all(attb.at[pl.ds(0, ny - 1)], ob_recv)

    def mix(h):
        columns = slice(h * HEAD_DIM, (h + 1) * HEAD_DIM)
        result = atta[h] if h < ha else attb[h - ha]
        out_ref[:, columns] = (
            hid[:, columns].astype(F32) + gates[:, columns] * result.astype(F32)
        ).astype(BF16)

    for h in range(ha, ha + ny):
        mix(h)
    wait_all(attb.at[pl.ds(0, ny - 1)], ob_send)
    wait_all(oa.at[pl.ds(0, ha - 1)], oa_send)
    wait_all(atta.at[pl.ds(0, ha - 1)], oa_recv)
    for h in range(ha):
        mix(h)


def per_device(
    ny, nx, hidden, queries, key_rows, values, query_gain, key_gain, gate_table, segment, text_count
):
    tok, width = hidden.shape
    requests = text_count.shape[0]
    ha = nx * CORES
    row_tok, col_tok = ha * tok, ny * tok
    anywhere = pl.BlockSpec(memory_space=pltpu.HBM)
    vmem = pl.BlockSpec(memory_space=pltpu.VMEM)
    smem = pl.BlockSpec(memory_space=pltpu.SMEM)
    dma = pltpu.SemaphoreType.DMA
    heads = (tok, HEAD_DIM)
    square = (LANES, LANES)
    a_rows, b_rows = row_tok // LANES, col_tok // LANES
    bufs = [
        ((tok, width), BF16),
        ((tok, width), BF16),
        ((tok, width), BF16),
        ((tok, width), BF16),
        ((requests, 2, width), BF16),
        ((ha, *heads), BF16),
        ((ha, *heads), BF16),
        ((ny, *heads), BF16),
        ((ny, *heads), BF16),
        ((ny, a_rows, *square), BF16),
        ((ny, ha, *heads), BF16),
        ((ha, b_rows, *square), BF16),
        ((ha, ny, *heads), BF16),
        ((row_tok, 2 * HEAD_DIM), BF16),
        ((col_tok, 2 * HEAD_DIM), BF16),
        ((ha, 1, LANES), F32),
        ((ny, 8, LANES), F32),
        ((ny, 8, LANES), F32),
        ((b_rows, LANES // tok, 8, LANES), F32),
        ((row_tok, row_tok), BF16),
        ((ny * requests, row_tok), BF16),
        ((row_tok, LANES), F32),
        ((2, *square), F32),
        ((tok, width), F32),
        ((2 * HEAD_DIM, 2 * max(row_tok, 2 * col_tok)), BF16),
        ((row_tok, row_tok), BF16),
        ((row_tok, LANES), F32),
        ((row_tok, LANES), F32),
        ((row_tok, HEAD_DIM), F32),
        ((col_tok, LANES), F32),
        ((col_tok, LANES), F32),
        ((col_tok, HEAD_DIM), F32),
        ((ha, *heads), BF16),
        ((ny, *heads), BF16),
        ((ha, *heads), BF16),
        ((ny, *heads), BF16),
    ]
    steps_y, steps_x = ny // 2, nx // 2
    sems = [(5,), (), (), (), (), (3,), (3,), (3,), (3,)]
    sems += [(2,), (2, 2, steps_y), (2,), (2, 2, steps_x), (2,), (2, 1 + 2 * steps_x), (), (), (), ()]
    return pl.pallas_call(
        functools.partial(kernel, ny, nx, tok, requests),
        out_shape=jax.ShapeDtypeStruct((tok, width), BF16),
        in_specs=[anywhere] * 4 + [vmem] * 2 + [anywhere] + [smem] * 2,
        out_specs=vmem,
        scratch_shapes=[pltpu.VMEM(*buf) for buf in bufs] + [dma(sem) if sem else dma for sem in sems],
        compiler_params=pltpu.CompilerParams(
            collective_id=0, has_side_effects=True, vmem_limit_bytes=VMEM_BYTES
        ),
        name="joint_attention",
    )(hidden, queries, key_rows, values, query_gain, key_gain, gate_table, segment, text_count)


def solution(mesh):
    groups, seq = mesh.shape["groups"], mesh.shape["seq"]
    nx = math.isqrt(seq // CORES)
    ny = seq // CORES // nx
    finer = Mesh(mesh.devices.reshape(groups, ny, nx, CORES), GROUPS_SEQ)
    placed = (
        P(GROUPS_SEQ, None),
        P(GROUPS_SEQ, None),
        P(GROUPS_SEQ, None),
        P(GROUPS_SEQ, None),
        P(),
        P(),
        P("groups", None, None),
        P(GROUPS_SEQ),
        P("groups"),
    )
    return jax.shard_map(
        functools.partial(per_device, ny, nx),
        mesh=finer,
        in_specs=placed,
        out_specs=P(GROUPS_SEQ, None),
        check_vma=False,
    )
```

time: 148 us -> 64.5 us (0.44)
  Pallas kernels: 0 us -> 62.7 us
  waiting for transfers between devices: 47 us -> 0 us
  starting transfers between devices: 44.9 us -> 0 us
  blocking collectives: 29.5 us -> 0 us
  local copies, waits for them, and re-layouts: 12.6 us -> 1.62 us
  other arithmetic: 7.28 us -> 0 us
  matrix products: 5.29 us -> 0 us
    pallas_call x0 -> x1, Pallas kernels: none -> 62.7 us  [per_device(): pl.pallas_call(functools.partial(kernel, ny, nx, tok, requests), out_shap...]
    all_to_all x3 -> x0, waiting for transfers between devices: 47 us -> none  [the longest x1 30.8 us: per_device(): lax.all_to_all(outgoing, SEQ, split_axis=0, concat_axis=0, tiled=True)]
    all_to_all x3 -> x0, starting transfers between devices: 44.9 us -> none  [the longest x1 27.4 us: per_device(): lax.all_to_all(segment_out, SEQ, split_axis=0, concat_axis=0, tiled=True)]
    unnamed x1 -> x0, blocking collectives: 22.4 us -> none
    all_gather x1 -> x0, blocking collectives: 7.09 us -> none  [gather_in_order(): parts = lax.all_gather(parts, axes[k])]
    gather x6 -> x0, local copies, waits for them, and re-layouts: 3.92 us -> none  [the longest x1 1.43 us: per_device(): jnp.take(segment, bucket_index, axis=0, mode='fill', fill_value=-1)]
    sub x1 -> x0, matrix products: 3.02 us -> none  [attend(): weights = jnp.exp(scores - largest)]
    select_n x5 -> x0, other arithmetic: 2.44 us -> none  [the longest x2 1.65 us: per_device(): jnp.take(stacked, bucket_index, axis=1, mode='fill', fill_value=0)]
  transfers between devices with their start and end apart: 3 -> 0, of which waited for: 2 -> 0; matrix products, arithmetic and copies ran while one was open for 7% -> 0% of each run, Pallas kernels for 0% -> 0%
where the time goes in v2:
time: 64.5 us; the launch traced here: 64.4 us
  Pallas kernels  62.7 us (97%)
  local copies, waits for them, and re-layouts  1.62 us (3%)
    pallas_call x1, Pallas kernels, per_device(): pl.pallas_call(functools.partial(kernel, ny, nx, tok, requests), out_shap...  62.7 us
    unnamed x1, local copies, waits for them, and re-layouts  1.62 us

profile of v2, /device:TPU:513, one launch (start us, length us, event | category | flops | bytes accessed | tf_op | source)
XLA Modules:
  0.0 64.4 jit_solution(3633843310328365561)
XLA Ops:
  0.0 62.7 %joint_attention.1 = bf16[32,3072]{1,0:T(8,128)(2,1)} custom-call(bf16[32,3072]{1,0:T(8,128)(2,1)} %hidden_hbm.1, bf16[32,3072]{1,0:T(8,128)(2,1)} %query_hbm.1, bf16[32,3072]{1,0:T(8,128)(2,1)} %key_hbm.1, bf16[32,3072]{1,0:T(8,128)(2,1)} %value_hbm.1, f32[2,128]{1,0:T(2,128)} %query_gain.1, f32[2,128]{1,0:T(2,128)} %key_gain.1, ...), custom_call_target="tpu_custom_call" | custom-call | tf_op jit(solution)/shard_map/joint_attention/pallas_call | solution.py:486
  62.8 1.6 %copy.11 = bf16[32,3072]{1,0:T(8,128)(2,1)} copy(bf16[32,3072]{1,0:T(8,128)(2,1)} %joint_attention.1) | data formatting | bytes 393216

commit v3 on v2

--- a/solution.py
+++ b/solution.py
@@ -17,7 +17,7 @@
 SAME = (128.0, 64.0)
 LATER = 64.0
 BLOCK = 256
-VMEM_BYTES = 60 * 1024 * 1024
+VMEM_BYTES = 40 * 1024 * 1024
 Y, X, C = "seq_0", "seq_1", "seq_2"
 GROUPS_SEQ = ("groups", Y, X, C)
 MESH = pl.DeviceIdType.MESH
@@ -27,9 +27,9 @@
 
 def kernel(
     ny, nx, tok, requests,
-    hidden_hbm, query_hbm, key_hbm, value_hbm, query_gain, key_gain, gate_hbm, seg_ref, text_ref,
+    hidden_hbm, query_hbm, key_hbm, value_hbm, query_gain_hbm, key_gain_hbm, gate_hbm, seg_hbm, text_hbm,
     out_ref,
-    hid, que, key, val, gat,
+    hid, que, key, val, gat, kinds, query_gain, key_gain, seg_ref, text_ref,
     kra, qra, krb, qrb, ka, va, kb, vb, qa, qb,
     segrow, segall, codea, codeb, tri, hot, cola, gains, gates, kwork, held,
     ma, la, acca, mb, lb, accb, oa, ob, atta, attb,
@@ -48,7 +48,17 @@
     loads = [
         pltpu.make_async_copy(src, dst, load_sem.at[n])
         for n, (src, dst) in enumerate(
-            [(key_hbm, key), (value_hbm, val), (query_hbm, que), (hidden_hbm, hid), (gate_hbm, gat)]
+            [
+                (key_hbm, key),
+                (value_hbm, val),
+                (query_hbm, que),
+                (seg_hbm, seg_ref),
+                (text_hbm, text_ref),
+                (key_gain_hbm, key_gain),
+                (query_gain_hbm, query_gain),
+                (gate_hbm, gat),
+                (hidden_hbm, hid),
+            ]
         )
     ]
     for load in loads:
@@ -58,14 +68,14 @@
         return lax.rem(a + 2 * n, n)
 
     row = []
-    for dx in range(nx):
+    for dx in sorted(range(nx), key=lambda d: -min(d, nx - d)):
         for dc in range(CORES):
             if dx or dc:
                 xx = around(x + dx, nx)
                 cc = c if dc == 0 else 1 - c
                 row.append((xx * CORES + cc, {Y: y, X: xx, C: cc}))
     col = []
-    for dy in range(1, ny):
+    for dy in sorted(range(1, ny), key=lambda d: -min(d, ny - d)):
         yy = around(y + dy, ny)
         col.append((yy, {Y: yy, X: x, C: c}))
     partner = {Y: y, X: x, C: 1 - c}
@@ -74,6 +84,7 @@
     for _, dev in row + col:
         pl.semaphore_signal(barrier, inc=1, device_id=dev, device_id_type=MESH)
 
+    loads[3].wait()
     lane = lax.broadcasted_iota(jnp.int32, (1, LANES), 1)
     lane_f = lane.astype(F32)
     place = lax.rem(lane, tok)
@@ -81,6 +92,45 @@
     for i in range(tok):
         mine = jnp.where(place == i, seg_ref[i].astype(F32), mine)
     segrow[pl.ds(idx, 1)] = mine.reshape(1, 1, LANES)
+    loads[0].wait()
+    pl.semaphore_wait(barrier, len(row) + len(col))
+
+    def remote(src, dst, send, recv, dev):
+        return pltpu.make_async_remote_copy(
+            src_ref=src, dst_ref=dst, send_sem=send, recv_sem=recv, device_id=dev, device_id_type=MESH
+        )
+
+    def head(ref, h):
+        return ref.at[:, pl.ds(pl.multiple_of(h * HEAD_DIM, HEAD_DIM), HEAD_DIM)]
+
+    def head_value(ref, h):
+        return ref[:, pl.ds(pl.multiple_of(h * HEAD_DIM, HEAD_DIM), HEAD_DIM)]
+
+    def wait_all(ref, sem):
+        pltpu.make_async_copy(ref, ref, sem).wait()
+
+    tensors = (key, val, que)
+    a_in = (kra, va.at[y], qra)
+    b_in = (krb, vb.at[idx], qrb)
+
+    def a_start(n):
+        for j, dev in row:
+            remote(head(tensors[n], j), a_in[n].at[idx], a_send.at[n], a_recv.at[n], dev).start()
+
+    def b_start(n):
+        for j, dev in col:
+            remote(head(tensors[n], ha + j), b_in[n].at[y], b_send.at[n], b_recv.at[n], dev).start()
+
+    a_start(0)
+    b_start(0)
+    for _, dev in row:
+        remote(segrow.at[idx], segrow.at[idx], seg_send, seg_recv, dev).start()
+    for n in (1, 2):
+        loads[n].wait()
+        b_start(n)
+
+    for load in loads[4:8]:
+        load.wait()
     down = lax.broadcasted_iota(jnp.int32, (requests, LANES), 0)
     limit = jnp.zeros((requests, LANES), F32)
     for i in range(requests):
@@ -102,42 +152,8 @@
         l[...] = jnp.zeros(l.shape, F32)
         acc[...] = jnp.zeros(acc.shape, F32)
 
-    loads[0].wait()
-    pl.semaphore_wait(barrier, len(row) + len(col))
-
-    def remote(src, dst, send, recv, dev):
-        return pltpu.make_async_remote_copy(
-            src_ref=src, dst_ref=dst, send_sem=send, recv_sem=recv, device_id=dev, device_id_type=MESH
-        )
-
-    def head(ref, h):
-        return ref.at[:, pl.ds(pl.multiple_of(h * HEAD_DIM, HEAD_DIM), HEAD_DIM)]
-
-    def head_value(ref, h):
-        return ref[:, pl.ds(pl.multiple_of(h * HEAD_DIM, HEAD_DIM), HEAD_DIM)]
-
-    def wait_all(ref, sem):
-        pltpu.make_async_copy(ref, ref, sem).wait()
-
-    tensors = (key, val, que)
-    a_in = (kra, va.at[y], qra)
-    b_in = (krb, vb.at[idx], qrb)
-
-    def a_start(n):
-        for j, dev in row:
-            remote(head(tensors[n], j), a_in[n].at[idx], a_send.at[n], a_recv.at[n], dev).start()
-
-    def b_start(n):
-        for j, dev in col:
-            remote(head(tensors[n], ha + j), b_in[n].at[y], b_send.at[n], b_recv.at[n], dev).start()
-
-    a_start(0)
-    for _, dev in row:
-        remote(segrow.at[idx], segrow.at[idx], seg_send, seg_recv, dev).start()
-    for n in range(3):
-        if n:
-            loads[n].wait()
-        b_start(n)
+    for kind in range(2):
+        kinds[kind] = gat[:, kind, :]
 
     kra[pl.ds(idx, 1)] = head_value(key, idx)[None]
     qra[pl.ds(idx, 1)] = head_value(que, idx)[None]
@@ -153,19 +169,26 @@
             return ref.at[:, pl.ds(way * (HEAD_DIM // 2), HEAD_DIM // 2)]
         return ref.at[pl.ds(way * (count // 2), count // 2)]
 
-    def a_part(t, slot, way, s):
-        part = (ka, va)[t].at[slot]
-        return part if s < full else half(part, t, way, ha)
-
     def b_part(t, slot, way, s):
         part = (kb, vb)[t].at[slot]
         return part if s < full_x else half(part, t, way, ny)
 
     def a_ring(t, way, s, back):
         sign = 1 - 2 * way
-        part = a_part(t, around(y - sign * back, ny), way, s)
+        slot = around(y - sign * back, ny)
+        if t == 0:
+            part = ka.at[slot] if s < full else half(ka.at[slot], 0, way, ha)
+        else:
+            part = half(va.at[slot], 1, t - 1, ha)
         dev = {Y: around(y + sign, ny), X: x, C: c}
-        return remote(part, part, ra_send.at[t], ra_recv.at[t, way, s], dev)
+        return remote(part, part, ra_send.at[min(t, 1)], ra_recv.at[t, way, s], dev)
+
+    def a_takes(t, way, s):
+        return s < full or t == 0 or t - 1 == way
+
+    def a_first(t):
+        for way in ways:
+            a_ring(t, way, 0, 0).start()
 
     def b_ring(t, way, s, back):
         sign = 1 - 2 * way
@@ -188,8 +211,9 @@
 
     def a_pass(t, s):
         for way in ways:
-            a_ring(t, way, s, s + 1).wait_recv()
-            if s < full:
+            if a_takes(t, way, s):
+                a_ring(t, way, s, s + 1).wait_recv()
+            if s < full and a_takes(t, way, s + 1):
                 a_ring(t, way, s + 1, s + 1).start()
 
     def b_pass(t, s):
@@ -201,14 +225,20 @@
 
     wait_all(kra.at[peers_a], a_send.at[0])
     a_start(1)
+    wait_all(kra.at[peers_a], a_recv.at[0])
+    for r in range(a_rows):
+        ka[pl.ds(y, 1), r : r + 1] = turned(kra[r * per : (r + 1) * per])[None, None]
+    a_first(0)
+    wait_all(kra.at[peers_a], a_send.at[1])
+    a_start(2)
     wait_all(krb.at[peers_b], b_recv.at[0])
     for r in range(b_rows):
         kb[pl.ds(idx, 1), r : r + 1] = turned(krb[r * per : (r + 1) * per])[None, None]
-    wait_all(kra.at[peers_a], a_recv.at[0])
-    for r in range(a_rows):
-        ka[pl.ds(y, 1), r : r + 1] = turned(kra[r * per : (r + 1) * per])[None, None]
-    for way in ways:
-        a_ring(0, way, 0, 0).start()
+    wait_all(vb.at[0, peers_b], b_recv.at[1])
+    for t in (0, 1):
+        for way in ways:
+            b_ring(t, way, 0, 0).start()
+        d_copy(t, 0, -1, c).start()
     wait_all(segrow.at[peers_a], seg_recv)
     for r in range(a_rows):
         joined = segrow[per * r]
@@ -217,18 +247,8 @@
         segall[pl.ds(y, 1), r : r + 1, :] = joined[None]
     for _, dev in col:
         remote(segall.at[y], segall.at[y], all_send, all_recv, dev).start()
-    wait_all(kra.at[peers_a], a_send.at[1])
-    for way in ways:
-        b_ring(0, way, 0, 0).start()
-    d_copy(0, 0, -1, c).start()
-    wait_all(vb.at[0, peers_b], b_recv.at[1])
-    for way in ways:
-        b_ring(1, way, 0, 0).start()
-    d_copy(1, 0, -1, c).start()
-    a_start(2)
     wait_all(va.at[0, peers_a], a_recv.at[1])
-    for way in ways:
-        a_ring(1, way, 0, 0).start()
+    a_first(1)
     a_pass(0, 0)
     wait_all(segall.at[peers_b], all_recv)
     for yy in range(ny):
@@ -310,9 +330,16 @@
     def blocks_a(slots):
         return [(ka[slot, r], code_a(slot, r)) for slot in slots for r in range(a_rows)]
 
-    def attend_a(slots):
+    def keys_a(slots):
+        count = key_work(blocks_a(slots))
+        step = min(BLOCK, row_tok)
+        for b in range(row_tok // step):
+            rows = slice(b * step, (b + 1) * step)
+            held[rows, : count * LANES], acca[rows, :] = soften(qa, ma, la, acca, count, rows)
+
+    def values_a(slots, rows=slice(None)):
         vals = jnp.concatenate([va[slot].reshape(row_tok, HEAD_DIM) for slot in slots], axis=0)
-        attend(qa, ma, la, acca, blocks_a(slots), vals)
+        return acca[rows, :] + jnp.dot(held[rows, : vals.shape[0]], vals, preferred_element_type=F32)
 
     def attend_b(places):
         ids = [place * CORES + core for place in places for core in range(CORES)]
@@ -333,8 +360,7 @@
             return [around(x - s - 1, nx), around(x + s + 1, nx)]
         return [around(x + nx // 2, nx)]
 
-    b_pass(0, 0)
-    b_pass(1, 0)
+    a_first(2)
     wait_all(qrb.at[peers_b], b_recv.at[2])
     wait_all(qra.at[peers_a], a_recv.at[2])
     for r in range(a_rows):
@@ -343,43 +369,54 @@
     for r in range(b_rows):
         part = slice(r * LANES, (r + 1) * LANES)
         qb[part, :], _ = query(qrb[r * per : (r + 1) * per], code_b(idx, r))
-    attend_a([y])
-    a_pass(1, 0)
-    attend_b(b_slots(-1))
-
-    for load in loads[3:]:
-        load.wait()
-    code = cola[pl.ds(pl.multiple_of(idx * tok, tok), tok), :]
-    late = code >= LATER
-    seg = jnp.where(late, code - LATER, code)
-    total = None
-    for kind in range(2):
-        pick = jnp.where((seg == lane_f) & (late == (kind == 1)), 1.0, 0.0).astype(BF16)[:, :requests]
-        term = jnp.dot(pick, gat[:, kind, :], preferred_element_type=F32)
-        total = term if total is None else total + term
-    gates[...] = total
-
-    b_step, b_done = 1, -1
-    for s in range(full):
-        if s + 1 < full:
-            a_pass(0, s + 1)
+    keys_a([y])
+    acca[...] = values_a([y])
+    b_pass(0, 0)
+    b_pass(1, 0)
+
+    b_step, b_done = 1, -2
+
+    def b_next():
         if b_step <= full_x:
             b_pass(0, b_step)
             b_pass(1, b_step)
-            b_step += 1
-        attend_a([around(y - s - 1, ny), around(y + s + 1, ny)])
-        if s + 1 < full:
-            a_pass(1, s + 1)
-        if b_done + 1 < b_step:
-            b_done += 1
-            places = b_slots(b_done)
+        return b_step + 1
+
+    def b_attend(upto):
+        for b in range(b_done + 1, upto + 1):
+            places = b_slots(b)
             attend_b(places)
-    for s in range(b_step, full_x + 1):
-        b_pass(0, s)
-        b_pass(1, s)
-    for s in range(b_done + 1, full_x + 1):
-        places = b_slots(s)
-        attend_b(places)
+        return max(b_done, upto)
+
+    for s in range(full):
+        slots = [around(y - s - 1, ny), around(y + s + 1, ny)]
+        final = s + 1 == full
+        if not final:
+            a_pass(0, s + 1)
+        a_pass(1, s)
+        keys_a(slots)
+        a_pass(2, s)
+        if s > 0:
+            b_step = b_next()
+        acca[...] = values_a(slots)
+        if not final:
+            b_done = b_attend(min(s, full_x))
+        if s == 0 and not final:
+            b_step = b_next()
+        if s == 0:
+            loads[8].wait()
+            code = cola[pl.ds(pl.multiple_of(idx * tok, tok), tok), :]
+            late = code >= LATER
+            seg = jnp.where(late, code - LATER, code)
+            total = 0.0
+            for kind in range(2):
+                pick = jnp.where((seg == lane_f) & (late == (kind == 1)), 1.0, 0.0).astype(BF16)[:, :requests]
+                total = total + jnp.dot(pick, kinds[kind], preferred_element_type=F32)
+            gates[...] = total
+
+    while b_step <= full_x:
+        b_step = b_next()
+    b_done = b_attend(full_x)
 
     ob[...] = finish(lb[...], accb[...]).reshape(ny, tok, HEAD_DIM)
     for j, dev in col:
@@ -388,14 +425,10 @@
 
     a_pass(0, full)
     last = around(y + ny // 2, ny)
-    count = key_work(blocks_a([last]))
-    for b in range(a_rows):
-        rows = slice(b * LANES, (b + 1) * LANES)
-        held[rows, :], acca[rows, :] = soften(qa, ma, la, acca, count, rows)
+    keys_a([last])
     a_pass(1, full)
-    oa[...] = finish(
-        la[...], acca[...] + jnp.dot(held[...], va[last].reshape(row_tok, HEAD_DIM), preferred_element_type=F32)
-    ).reshape(ha, tok, HEAD_DIM)
+    a_pass(2, full)
+    oa[...] = finish(la[...], values_a([last])).reshape(ha, tok, HEAD_DIM)
     for j, dev in row:
         remote(oa.at[j], atta.at[idx], oa_send, oa_recv, dev).start()
     atta[pl.ds(idx, 1)] = oa[pl.ds(idx, 1)]
@@ -437,7 +470,6 @@
     row_tok, col_tok = ha * tok, ny * tok
     anywhere = pl.BlockSpec(memory_space=pltpu.HBM)
     vmem = pl.BlockSpec(memory_space=pltpu.VMEM)
-    smem = pl.BlockSpec(memory_space=pltpu.SMEM)
     dma = pltpu.SemaphoreType.DMA
     heads = (tok, HEAD_DIM)
     square = (LANES, LANES)
@@ -448,6 +480,9 @@
         ((tok, width), BF16),
         ((tok, width), BF16),
         ((requests, 2, width), BF16),
+        ((2, requests, width), BF16),
+        ((2, HEAD_DIM), F32),
+        ((2, HEAD_DIM), F32),
         ((ha, *heads), BF16),
         ((ha, *heads), BF16),
         ((ny, *heads), BF16),
@@ -468,7 +503,7 @@
         ((2, *square), F32),
         ((tok, width), F32),
         ((2 * HEAD_DIM, 2 * max(row_tok, 2 * col_tok)), BF16),
-        ((row_tok, row_tok), BF16),
+        ((row_tok, 2 * row_tok), BF16),
         ((row_tok, LANES), F32),
         ((row_tok, LANES), F32),
         ((row_tok, HEAD_DIM), F32),
@@ -481,19 +516,28 @@
         ((ny, *heads), BF16),
     ]
     steps_y, steps_x = ny // 2, nx // 2
-    sems = [(5,), (), (), (), (), (3,), (3,), (3,), (3,)]
-    sems += [(2,), (2, 2, steps_y), (2,), (2, 2, steps_x), (2,), (2, 1 + 2 * steps_x), (), (), (), ()]
+    sems = [(9,), (), (), (), (), (3,), (3,), (3,), (3,)]
+    sems += [(2,), (3, 2, steps_y), (2,), (2, 2, steps_x), (2,), (2, 1 + 2 * steps_x), (), (), (), ()]
+    inputs = [
+        pltpu.with_memory_space_constraint(array, pltpu.HBM)
+        for array in (
+            hidden, queries, key_rows, values, query_gain, key_gain, gate_table, segment, text_count
+        )
+    ]
     return pl.pallas_call(
         functools.partial(kernel, ny, nx, tok, requests),
         out_shape=jax.ShapeDtypeStruct((tok, width), BF16),
-        in_specs=[anywhere] * 4 + [vmem] * 2 + [anywhere] + [smem] * 2,
+        in_specs=[anywhere] * 9,
         out_specs=vmem,
-        scratch_shapes=[pltpu.VMEM(*buf) for buf in bufs] + [dma(sem) if sem else dma for sem in sems],
+        scratch_shapes=[pltpu.VMEM(*buf) for buf in bufs[:8]]
+        + [pltpu.SMEM((tok,), jnp.int32), pltpu.SMEM((requests,), jnp.int32)]
+        + [pltpu.VMEM(*buf) for buf in bufs[8:]]
+        + [dma(sem) if sem else dma for sem in sems],
         compiler_params=pltpu.CompilerParams(
             collective_id=0, has_side_effects=True, vmem_limit_bytes=VMEM_BYTES
         ),
         name="joint_attention",
-    )(hidden, queries, key_rows, values, query_gain, key_gain, gate_table, segment, text_count)
+    )(*inputs)
 
 
 def solution(mesh):

time: 64.5 us -> 60.7 us (0.941)
  Pallas kernels: 62.7 us -> 59.9 us
  local copies, waits for them, and re-layouts: 1.62 us -> 0.68 us
    pallas_call x1, Pallas kernels: 62.7 us -> 59.9 us  [per_device(): pl.pallas_call(functools.partial(kernel, ny, nx, tok, requests), out_shap...]
    unnamed x1, local copies, waits for them, and re-layouts: 1.62 us -> 0.68 us
where the time goes in v3:
time: 60.7 us; the launch traced here: 60.6 us
  Pallas kernels  59.9 us (99%)
  local copies, waits for them, and re-layouts  0.68 us (1%)
    pallas_call x1, Pallas kernels, per_device(): pl.pallas_call(functools.partial(kernel, ny, nx, tok, requests), out_shap...  59.9 us

profile of v3, /device:TPU:513, one launch (start us, length us, event | category | flops | bytes accessed | tf_op | source)
XLA Modules:
  0.0 60.6 jit_solution(6365466280816298331)
XLA Ops:
  0.0 59.9 %joint_attention.1 = bf16[32,3072]{1,0:T(8,128)(2,1)S(1)} custom-call(bf16[32,3072]{1,0:T(8,128)(2,1)} %hidden_hbm.1, bf16[32,3072]{1,0:T(8,128)(2,1)} %query_hbm.1, bf16[32,3072]{1,0:T(8,128)(2,1)} %key_hbm.1, bf16[32,3072]{1,0:T(8,128)(2,1)} %value_hbm.1, f32[2,128]{1,0:T(2,128)} %query_gain_hbm.1, f32[2,128]{1,0:T(2,128)} %key_gain_hbm.1, ...), custom_call_target="tpu_custom_call" | custom-call | tf_op jit(solution)/shard_map/joint_attention/pallas_call | solution.py:527
  59.9 0.7 %copy.11 = bf16[32,3072]{1,0:T(8,128)(2,1)} copy(bf16[32,3072]{1,0:T(8,128)(2,1)S(1)} %joint_attention.1) | data formatting | bytes 393216

commit v4 on v3

--- a/solution.py
+++ b/solution.py
@@ -176,19 +176,20 @@
     def a_ring(t, way, s, back):
         sign = 1 - 2 * way
         slot = around(y - sign * back, ny)
-        if t == 0:
-            part = ka.at[slot] if s < full else half(ka.at[slot], 0, way, ha)
-        else:
-            part = half(va.at[slot], 1, t - 1, ha)
+        part = half((ka, va)[t // 2].at[slot], t // 2, t % 2, ha)
         dev = {Y: around(y + sign, ny), X: x, C: c}
-        return remote(part, part, ra_send.at[min(t, 1)], ra_recv.at[t, way, s], dev)
+        return remote(part, part, ra_send.at[t], ra_recv.at[t, way, s], dev)
 
     def a_takes(t, way, s):
-        return s < full or t == 0 or t - 1 == way
+        return s < full or t % 2 == way
 
     def a_first(t):
         for way in ways:
             a_ring(t, way, 0, 0).start()
+
+    def a_left(t, halves):
+        size = ha // 2 * tok * HEAD_DIM // held.shape[1]
+        wait_all(held.at[pl.ds(0, halves * size)], ra_send.at[t])
 
     def b_ring(t, way, s, back):
         sign = 1 - 2 * way
@@ -239,6 +240,7 @@
         for way in ways:
             b_ring(t, way, 0, 0).start()
         d_copy(t, 0, -1, c).start()
+    a_first(1)
     wait_all(segrow.at[peers_a], seg_recv)
     for r in range(a_rows):
         joined = segrow[per * r]
@@ -248,8 +250,10 @@
     for _, dev in col:
         remote(segall.at[y], segall.at[y], all_send, all_recv, dev).start()
     wait_all(va.at[0, peers_a], a_recv.at[1])
-    a_first(1)
+    a_first(2)
     a_pass(0, 0)
+    a_pass(1, 0)
+    a_first(3)
     wait_all(segall.at[peers_b], all_recv)
     for yy in range(ny):
         for r in range(a_rows):
@@ -360,7 +364,6 @@
             return [around(x - s - 1, nx), around(x + s + 1, nx)]
         return [around(x + nx // 2, nx)]
 
-    a_first(2)
     wait_all(qrb.at[peers_b], b_recv.at[2])
     wait_all(qra.at[peers_a], a_recv.at[2])
     for r in range(a_rows):
@@ -393,14 +396,17 @@
         final = s + 1 == full
         if not final:
             a_pass(0, s + 1)
-        a_pass(1, s)
+            a_pass(1, s + 1)
+        a_pass(2, s)
         keys_a(slots)
-        a_pass(2, s)
-        if s > 0:
+        a_pass(3, s)
+        if s > 0 and not final:
             b_step = b_next()
         acca[...] = values_a(slots)
-        if not final:
-            b_done = b_attend(min(s, full_x))
+        if final:
+            while b_step <= full_x:
+                b_step = b_next()
+        b_done = b_attend(full_x if final else min(s, b_step - 1, full_x))
         if s == 0 and not final:
             b_step = b_next()
         if s == 0:
@@ -414,20 +420,17 @@
                 total = total + jnp.dot(pick, kinds[kind], preferred_element_type=F32)
             gates[...] = total
 
-    while b_step <= full_x:
-        b_step = b_next()
-    b_done = b_attend(full_x)
-
     ob[...] = finish(lb[...], accb[...]).reshape(ny, tok, HEAD_DIM)
     for j, dev in col:
         remote(ob.at[j], attb.at[y], ob_send, ob_recv, dev).start()
     attb[pl.ds(y, 1)] = ob[pl.ds(y, 1)]
 
     a_pass(0, full)
+    a_pass(1, full)
     last = around(y + ny // 2, ny)
     keys_a([last])
-    a_pass(1, full)
     a_pass(2, full)
+    a_pass(3, full)
     oa[...] = finish(la[...], values_a([last])).reshape(ha, tok, HEAD_DIM)
     for j, dev in row:
         remote(oa.at[j], atta.at[idx], oa_send, oa_recv, dev).start()
@@ -438,8 +441,9 @@
     wait_all(kra.at[peers_a], a_send.at[2])
     for n in range(3):
         wait_all(krb.at[peers_b], b_send.at[n])
+    for t in range(4):
+        a_left(t, 2 * full + 1)
     for t in (0, 1):
-        wait_all((ka, va)[t].at[pl.ds(0, ny - 1)], ra_send.at[t])
         wait_all((kb, vb)[t].at[pl.ds(0, nx - 1)], rb_send.at[t])
         wait_all((kb, vb)[t].at[pl.ds(0, nx)], d_send.at[t])
 
@@ -517,7 +521,7 @@
     ]
     steps_y, steps_x = ny // 2, nx // 2
     sems = [(9,), (), (), (), (), (3,), (3,), (3,), (3,)]
-    sems += [(2,), (3, 2, steps_y), (2,), (2, 2, steps_x), (2,), (2, 1 + 2 * steps_x), (), (), (), ()]
+    sems += [(4,), (4, 2, steps_y), (2,), (2, 2, steps_x), (2,), (2, 1 + 2 * steps_x), (), (), (), ()]
     inputs = [
         pltpu.with_memory_space_constraint(array, pltpu.HBM)
         for array in (

time: 60.7 us -> 60 us (0.988)
  Pallas kernels: 59.9 us -> 59.2 us
    pallas_call x1, Pallas kernels: 59.9 us -> 59.2 us  [per_device(): pl.pallas_call(functools.partial(kernel, ny, nx, tok, requests), out_shap...]
where the time goes in v4:
time: 60 us; the launch traced here: 59.9 us
  Pallas kernels  59.2 us (99%)
  local copies, waits for them, and re-layouts  0.68 us (1%)
    pallas_call x1, Pallas kernels, per_device(): pl.pallas_call(functools.partial(kernel, ny, nx, tok, requests), out_shap...  59.2 us

profile of v4, /device:TPU:513, one launch (start us, length us, event | category | flops | bytes accessed | tf_op | source)
XLA Modules:
  0.0 59.9 jit_solution(774965160423095233)
XLA Ops:
  0.0 59.2 %joint_attention.1 = bf16[32,3072]{1,0:T(8,128)(2,1)S(1)} custom-call(bf16[32,3072]{1,0:T(8,128)(2,1)} %hidden_hbm.1, bf16[32,3072]{1,0:T(8,128)(2,1)} %query_hbm.1, bf16[32,3072]{1,0:T(8,128)(2,1)} %key_hbm.1, bf16[32,3072]{1,0:T(8,128)(2,1)} %value_hbm.1, f32[2,128]{1,0:T(2,128)} %query_gain_hbm.1, f32[2,128]{1,0:T(2,128)} %key_gain_hbm.1, ...), custom_call_target="tpu_custom_call" | custom-call | tf_op jit(solution)/shard_map/joint_attention/pallas_call | solution.py:531
  59.2 0.7 %copy.11 = bf16[32,3072]{1,0:T(8,128)(2,1)} copy(bf16[32,3072]{1,0:T(8,128)(2,1)S(1)} %joint_attention.1) | data formatting | bytes 393216
